TPU v7x, 32 devices: a whole 2x2x4 slice. The times are simulated.
32 devices in a mesh: dp: 8 (over z, core), mp: 4 (over y, x).
Axes of the slice: x: 2, y: 2, z: 4, core: 2. Of those that a mesh axis runs over, the one named last changes fastest.
Arguments:
- patches: bfloat16 [256, 256, 1280], P(('dp', 'mp')), may hold values from -6 to 6
- position: bfloat16 [256, 1280], replicated, may hold values from -3 to 3
- keep: int32 [256, 64], P(('dp', 'mp')), may hold values from 0 to 255, as said below
- counts: int32 [256], replicated, may hold values from 1 to 64, as said below
- offsets: int32 [256], replicated, may hold values from 0 to 10239, as said below
- ln_gain: float32 [1, 2, 1280], replicated, may hold values from 0.25 to 1.75
- ln_bias: float32 [1, 2, 1280], replicated, may hold values from -2 to 2
- w_qkv: bfloat16 [1, 3, 1280, 1280], P(None, None, 'dp', 'mp')
- b_qkv: float32 [1, 3, 1280], P(None, None, 'mp'), may hold values from -3 to 3
- w_o: bfloat16 [1, 1280, 1280], P(None, 'mp', 'dp'), may hold values from -0.15625 to 0.15625
- b_o: float32 [1, 1280], replicated, may hold values from -1.5 to 1.5
- w_up: bfloat16 [1, 1280, 5120], P(None, 'dp', 'mp'), may hold values from -0.15625 to 0.15625
- b_up: float32 [1, 5120], P(None, 'mp'), may hold values from -3 to 3
- w_down: bfloat16 [1, 5120, 1280], P(None, 'mp', 'dp'), may hold values from -0.078125 to 0.078125
- b_down: float32 [1, 1280], replicated, may hold values from -1.5 to 1.5
Outputs:
- encoded: bfloat16 [10240, 1280], P(('dp', 'mp'))
Inputs may be any that keep to these rules, and one draw needn't show every extreme that they name: `keep`: the first counts[i] entries of row i are distinct and name image i's visible patches; later entries are unused. `counts`: some image has exactly 64 visible patches. Image i, held by dp index s = i // 32, occupies packed rows offsets[i] to offsets[i] + counts[i] - 1, all inside the aligned block of 160 rows numbered d * 8 + s for some shard d; no two images share a row.
All inputs are finite; a program needn't handle non-finite values.
Results may differ from a plain program's by a relative error of at most 0.015.
Values may be sent and summed in bfloat16 or wider, within the bound.
A program may use at most 64 MiB of HBM per device.

v0:
```python
import functools
import math

import jax
import jax.numpy as jnp
from jax import lax
from jax.experimental import pallas as pl
from jax.experimental.pallas import tpu as pltpu
from jax.sharding import PartitionSpec as P

HEAD = 80
MESH = pl.DeviceIdType.MESH


def norm_rows(values, gain_row, shift_row):
    row_mean = jnp.mean(values, axis=-1, keepdims=True)
    centred = values - row_mean
    spread = jnp.mean(centred * centred, axis=-1, keepdims=True)
    return (centred * lax.rsqrt(spread + 1e-06) * gain_row + shift_row).astype(jnp.bfloat16)


def flip(index, mask, count):
    result = index
    bit = 1
    while bit < count:
        wanted = (mask // bit) % 2
        own = (index // bit) % 2
        result = result + bit * wanted * (1 - 2 * own)
        bit = bit * 2
    return result


def tile_of(extent, most):
    tile = most
    while extent % tile != 0:
        tile = tile // 2
    return tile


def route_kernel(
    shards,
    groups,
    packed_ref,
    gain_ref,
    shift_ref,
    stream_ref,
    normed_ref,
    out_ref,
    send_sem,
    recv_sem,
    own_sem,
):
    per = shards // groups
    dp = lax.axis_index("dp")
    mp = lax.axis_index("mp")
    home = dp // per
    slot = lax.rem(dp, per) * groups + mp

    barrier = pltpu.get_barrier_semaphore()
    for j in range(per):
        for g in range(groups):
            source = mp * per + j

            @pl.when(jnp.logical_or(source != dp, mp != g))
            def _():
                pl.semaphore_signal(barrier, inc=1, device_id=(source, g), device_id_type=MESH)

    is_home = home == mp

    @pl.when(is_home)
    def _():
        pl.semaphore_wait(barrier, shards - 1)

    @pl.when(jnp.logical_not(is_home))
    def _():
        pl.semaphore_wait(barrier, shards)

    def remote(step):
        dest = lax.rem(dp + step, shards)
        return pltpu.make_async_remote_copy(
            src_ref=packed_ref.at[dest],
            dst_ref=out_ref.at[slot],
            send_sem=send_sem.at[step],
            recv_sem=recv_sem.at[slot],
            device_id=(dest, home),
            device_id_type=MESH,
        )

    own = pltpu.make_async_copy(packed_ref.at[dp], out_ref.at[slot], own_sem)
    for step in range(1, shards):
        remote(step).start()

    @pl.when(is_home)
    def _():
        own.start()
        own.wait()

    @pl.when(jnp.logical_not(is_home))
    def _():
        remote(0).start()
        remote(0).wait_send()

    for step in range(1, shards):
        remote(step).wait_send()
    for j in range(per):
        for g in range(groups):
            source = mp * per + j

            @pl.when(jnp.logical_or(source != dp, mp != g))
            def _():
                pltpu.make_async_remote_copy(
                    src_ref=packed_ref.at[0],
                    dst_ref=out_ref.at[j * groups + g],
                    send_sem=send_sem.at[0],
                    recv_sem=recv_sem.at[j * groups + g],
                    device_id=(dp, mp),
                    device_id_type=MESH,
                ).wait_recv()

    rows_tile = tile_of(packed_ref.shape[1], 32)
    for j in range(per):

        def some(i, carry):
            rows = pl.ds(pl.multiple_of(i * rows_tile, rows_tile), rows_tile)
            whole = jnp.concatenate(
                [out_ref[j * groups + g, rows, :] for g in range(groups)], axis=-1
            )
            stream_ref[j, rows, :] = whole
            normed_ref[j, rows, :] = norm_rows(
                whole.astype(jnp.float32), gain_ref[...], shift_ref[...]
            )
            return carry

        lax.fori_loop(0, packed_ref.shape[1] // rows_tile, some, 0)


def route(packed, gain_row, shift_row, shards, groups):
    slot_rows, width = packed.shape[1:]
    result = jax.ShapeDtypeStruct((shards // groups, slot_rows, width * groups), packed.dtype)
    vmem = pl.BlockSpec(memory_space=pltpu.VMEM)
    return pl.pallas_call(
        functools.partial(route_kernel, shards, groups),
        out_shape=(result, result),
        in_specs=[vmem] * 3,
        out_specs=(vmem, vmem),
        scratch_shapes=[
            pltpu.VMEM(packed.shape, packed.dtype),
            pltpu.SemaphoreType.DMA((shards,)),
            pltpu.SemaphoreType.DMA((shards,)),
            pltpu.SemaphoreType.DMA,
        ],
        compiler_params=pltpu.CompilerParams(collective_id=0, has_side_effects=True),
        cost_estimate=pl.CostEstimate(flops=15_000_000_000, bytes_accessed=0, transcendentals=0),
        name="route",
    )(packed, gain_row, shift_row)


def exchange(groups, x_ref, blocks, parts, backs, relay, sems, block_step, finish):
    own_sem, send_a, recv_a, send_b, recv_b = sems
    dp = lax.axis_index("dp")
    mp = lax.axis_index("mp")
    pieces = x_ref.shape[0]
    square = groups == 4 and pieces == 2
    partners = range(1, 3) if square else range(1, groups)

    barrier = pltpu.get_barrier_semaphore()
    for k in partners:
        pl.semaphore_signal(
            barrier, inc=1, device_id=(dp, flip(mp, k, groups)), device_id_type=MESH
        )
    own = pltpu.make_async_copy(x_ref, blocks.at[pl.ds(0, pieces)], own_sem)
    own.start()
    pl.semaphore_wait(barrier, len(partners))

    def send(source, target, out_sem, in_sem, k):
        return pltpu.make_async_remote_copy(
            src_ref=source,
            dst_ref=target,
            send_sem=out_sem,
            recv_sem=in_sem,
            device_id=(dp, flip(mp, k, groups)),
            device_id_type=MESH,
        )

    def out_copy(k, h):
        at = k * pieces + h
        return send(x_ref.at[h], blocks.at[at], send_a.at[at], recv_a.at[at], k)

    def back_copy(k, h):
        at = k * pieces + h
        return send(parts.at[at], backs.at[at], send_b.at[at], recv_b.at[at], k)

    if square:
        def forward(h):
            held, k = (2, 2) if h == 0 else (5, 1)
            at = 6 + h
            return send(blocks.at[held], blocks.at[at], send_a.at[at], recv_a.at[at], k)

        def across(h):
            at = 6 + h
            return send(parts.at[at], relay.at[h], send_b.at[at], recv_b.at[at], 1 + h)

        for k, h in ((1, 0), (2, 1), (1, 1), (2, 0)):
            out_copy(k, h).start()
        own.wait()

        def step(i, carry):
            late = (i + 2) // 8
            middle = ((i + 2) // 4) % 2
            k = middle * (1 + i % 2) + 3 * late
            h = (i // 4 + i % 2) % 2

            @pl.when(i == 2)
            def _():
                out_copy(1, 0).wait_recv()
                forward(0).start()
                out_copy(2, 1).wait_recv()
                forward(1).start()

            @pl.when(i >= 4)
            def _():
                out_copy(k, h).wait_recv()

            block_step(k * 2 + h, flip(mp, k, groups) * 2 + h)

            @pl.when(i == 2)
            def _():
                back_copy(1, 0).start()

            @pl.when(i == 3)
            def _():
                back_copy(2, 1).start()

            @pl.when(i == 6)
            def _():
                across(1).start()

            @pl.when(i == 7)
            def _():
                across(0).start()

            return carry

        lax.fori_loop(0, 8, step, 0)
        rows_tile = tile_of(x_ref.shape[1], 32)
        for h, k in ((1, 1), (0, 2)):
            across(h).wait_recv()

            def add(i, carry, h=h, k=k):
                rows = pl.ds(pl.multiple_of(i * rows_tile, rows_tile), rows_tile)
                parts[k * 2 + h, rows, :] = (
                    parts[k * 2 + h, rows, :].astype(jnp.float32)
                    + relay[h, rows, :].astype(jnp.float32)
                ).astype(jnp.bfloat16)
                return carry

            lax.fori_loop(0, x_ref.shape[1] // rows_tile, add, 0)
            back_copy(k, h).start()
        for k, h in ((1, 0), (2, 1), (1, 1), (2, 0)):
            back_copy(k, h).wait_recv()
        finish(partners)
        for h in range(2):
            forward(h).wait_send()
            across(h).wait_send()
            for k in partners:
                out_copy(k, h).wait_send()
                back_copy(k, h).wait_send()
        return

    for k in partners:
        for h in range(pieces):
            out_copy(k, h).start()
    own.wait()

    def step(i, carry):
        k = i // pieces
        h = i % pieces

        @pl.when(k > 0)
        def _():
            out_copy(k, h).wait_recv()

        block_step(i, flip(mp, k, groups) * pieces + h)

        @pl.when(k > 0)
        def _():
            back_copy(k, h).start()

        return carry

    lax.fori_loop(0, groups * pieces, step, 0)
    for k in partners:
        for h in range(pieces):
            back_copy(k, h).wait_recv()
    finish(partners)
    for k in partners:
        for h in range(pieces):
            out_copy(k, h).wait_send()
            back_copy(k, h).wait_send()


def finish_rows(x_ref, parts, backs, partners, write):
    pieces, row_count = x_ref.shape[:2]
    rows_tile = tile_of(row_count, 32)
    for h in range(pieces):

        def some(i, carry, h=h):
            rows = pl.ds(pl.multiple_of(i * rows_tile, rows_tile), rows_tile)
            total = parts[h, rows, :].astype(jnp.float32)
            for k in partners:
                total = total + backs[k * pieces + h, rows, :].astype(jnp.float32)
            write(h, rows, total)
            return carry

        lax.fori_loop(0, row_count // rows_tile, some, 0)


def attention_kernel(
    groups,
    x_ref,
    stream_ref,
    w_ref,
    b_ref,
    label_col_ref,
    label_row_ref,
    bias_ref,
    gain_ref,
    shift_ref,
    residual_ref,
    normed_ref,
    blocks,
    parts,
    backs,
    relay,
    attended_ref,
    *sems,
):
    row_count, depth = x_ref.shape[1:]
    width = w_ref.shape[2]
    heads = width // HEAD
    scale = 1.0 / math.sqrt(HEAD)
    tile = tile_of(depth, 256)

    def block_step(at_block, source):
        x = blocks[at_block]

        def project(t):
            y = jnp.dot(x, w_ref[t], preferred_element_type=jnp.float32)
            return (y + b_ref[t]).astype(jnp.bfloat16)

        query, key, value = project(0), project(1), project(2)
        matches = label_col_ref[source] == label_row_ref[source]
        lane_head = lax.broadcasted_iota(jnp.int32, (row_count, width), 1)
        total = jnp.zeros((row_count, width), jnp.float32)
        zero = jnp.zeros((row_count, width), jnp.bfloat16)
        for h in range(heads):
            inside = (lane_head >= h * HEAD) & (lane_head < (h + 1) * HEAD)
            scores = lax.dot_general(
                jnp.where(inside, query, zero),
                key,
                (((1,), (1,)), ((), ())),
                preferred_element_type=jnp.float32,
            )
            scores = jnp.where(matches, scores * scale, -jnp.inf)
            weights = jnp.exp(scores - jnp.max(scores, axis=-1, keepdims=True))
            inverse = 1.0 / jnp.sum(weights, axis=-1, keepdims=True)
            probabilities = (weights * inverse).astype(jnp.bfloat16)
            total = total + jnp.dot(
                probabilities, jnp.where(inside, value, zero), preferred_element_type=jnp.float32
            )
        attended_ref[...] = total.astype(jnp.bfloat16)

        def column(t, carry):
            at = pl.ds(pl.multiple_of(t * tile, tile), tile)
            parts[at_block, :, at] = lax.dot_general(
                attended_ref[...],
                w_ref[3, at, :],
                (((1,), (1,)), ((), ())),
                preferred_element_type=jnp.float32,
            ).astype(jnp.bfloat16)
            return carry

        lax.fori_loop(0, depth // tile, column, 0)

    def finish(partners):
        def write(h, rows, total):
            residual = stream_ref[h, rows, :].astype(jnp.float32) + total + bias_ref[...]
            residual_ref[h, rows, :] = residual
            normed_ref[h, rows, :] = norm_rows(residual, gain_ref[...], shift_ref[...])

        finish_rows(x_ref, parts, backs, partners, write)

    exchange(groups, x_ref, blocks, parts, backs, relay, sems, block_step, finish)


def mlp_kernel(
    groups,
    x_ref,
    residual_ref,
    up_ref,
    b_ref,
    down_ref,
    bias_ref,
    out_ref,
    blocks,
    parts,
    backs,
    relay,
    hidden_ref,
    *sems,
):
    row_count, depth = x_ref.shape[1:]
    width = up_ref.shape[1]
    tile = tile_of(depth, 256)
    up_tile = tile_of(width, 256)

    def block_step(at_block, source):
        def up(t, carry):
            at = pl.ds(pl.multiple_of(t * up_tile, up_tile), up_tile)
            y = jnp.dot(blocks[at_block], up_ref[:, at], preferred_element_type=jnp.float32) + b_ref[:, at]
            y = 0.5 * y * (1.0 + lax.erf(y * math.sqrt(0.5)))
            hidden_ref[:, at] = y.astype(jnp.bfloat16)
            return carry

        lax.fori_loop(0, width // up_tile, up, 0)

        def column(t, carry):
            at = pl.ds(pl.multiple_of(t * tile, tile), tile)
            parts[at_block, :, at] = lax.dot_general(
                hidden_ref[...],
                down_ref[at, :],
                (((1,), (1,)), ((), ())),
                preferred_element_type=jnp.float32,
            ).astype(jnp.bfloat16)
            return carry

        lax.fori_loop(0, depth // tile, column, 0)

    def finish(partners):
        def write(h, rows, total):
            out_ref[h, rows, :] = (residual_ref[h, rows, :] + total + bias_ref[...]).astype(
                jnp.bfloat16
            )

        finish_rows(x_ref, parts, backs, partners, write)

    exchange(groups, x_ref, blocks, parts, backs, relay, sems, block_step, finish)


def exchange_call(kernel, groups, args, outs, width, collective_id, name):
    pieces, row_count, depth = args[0].shape
    vmem = pl.BlockSpec(memory_space=pltpu.VMEM)
    many = pltpu.SemaphoreType.DMA((groups * pieces,))
    buffer = pltpu.VMEM((groups * pieces, row_count, depth), jnp.bfloat16)
    return pl.pallas_call(
        functools.partial(kernel, groups),
        out_shape=outs,
        in_specs=[vmem] * len(args),
        out_specs=jax.tree.map(lambda _: vmem, outs),
        scratch_shapes=[
            buffer,
            buffer,
            buffer,
            pltpu.VMEM((pieces, row_count, depth), jnp.bfloat16),
            pltpu.VMEM((row_count, width), jnp.bfloat16),
            pltpu.SemaphoreType.DMA,
            many,
            many,
            many,
            many,
        ],
        compiler_params=pltpu.CompilerParams(
            collective_id=collective_id, has_side_effects=True, vmem_limit_bytes=48 * 1024 * 1024
        ),
        cost_estimate=pl.CostEstimate(flops=50_000_000_000, bytes_accessed=0, transcendentals=0),
        name=name,
    )(*args)


def per_device(
    patches,
    position,
    keep,
    counts,
    offsets,
    ln_gain,
    ln_bias,
    w_qkv,
    b_qkv,
    w_o,
    b_o,
    w_up,
    b_up,
    w_down,
    b_down,
):
    local_images, patch_count, column_count = patches.shape
    keep_most = keep.shape[1]
    shard_count = lax.axis_size("dp")
    group_size = lax.axis_size("mp")
    images_here = local_images * group_size
    per_slot = (images_here + shard_count - 1) // shard_count
    slot_rows = max(keep_most + 16, per_slot * keep_most * 5 // 8)
    pack_rows = slot_rows * shard_count
    local_rows = pack_rows // group_size
    dp_index = lax.axis_index("dp")
    mp_index = lax.axis_index("mp")
    f32 = jnp.float32

    attention_shard = jnp.concatenate([w_qkv[0], w_o[0].T[None]], axis=0)
    w_attention = lax.all_gather(attention_shard, "dp", axis=1, tiled=True)

    chosen = (keep[:, :, None] == jnp.arange(patch_count, dtype=jnp.int32)).astype(jnp.bfloat16)
    tokens = (
        jnp.einsum("ijp,ipd->ijd", chosen, patches, preferred_element_type=f32)
        + jnp.einsum("ijp,pd->ijd", chosen, position, preferred_element_type=f32)
    ).astype(jnp.bfloat16)
    tokens, w_up_shard = lax.optimization_barrier((tokens, w_up[0]))
    w_up_full = lax.all_gather(w_up_shard, "dp", axis=0, tiled=True)

    first_image = dp_index * images_here
    group_counts = lax.dynamic_slice_in_dim(counts, first_image, images_here)
    group_offsets = lax.dynamic_slice_in_dim(offsets, first_image, images_here)
    positions_in = jnp.arange(keep_most, dtype=jnp.int32)
    group_live = positions_in[None, :] < group_counts[:, None]
    shard_index = group_offsets // pack_rows
    base_row = (
        shard_index * slot_rows + group_offsets - shard_index * pack_rows - dp_index * slot_rows
    )
    target = jnp.where(group_live, base_row[:, None] + positions_in[None, :], pack_rows).reshape(-1)
    image_ids = jnp.arange(counts.shape[0], dtype=jnp.int32)
    packed_rows = dp_index * pack_rows + jnp.arange(pack_rows, dtype=jnp.int32)
    inside = (packed_rows[:, None] >= offsets[None, :]) & (
        packed_rows[:, None] < (offsets + counts)[None, :]
    )
    labels = jnp.max(jnp.where(inside, image_ids[None, :] + 1, 0), axis=1) - 1

    featured = lax.all_to_all(
        tokens.reshape(-1, column_count), "mp", split_axis=1, concat_axis=0, tiled=True
    )
    featured, w_down_shard = lax.optimization_barrier((featured, w_down[0]))
    w_down_rows = lax.all_gather(w_down_shard, "dp", axis=1, tiled=True).T
    feature_count = featured.shape[1]
    placing = (jnp.arange(pack_rows, dtype=jnp.int32)[:, None] == target[None, :]).astype(
        jnp.bfloat16
    )
    packed = jnp.dot(placing, featured, preferred_element_type=f32).astype(jnp.bfloat16)
    stream, normed = route(
        packed.reshape(shard_count, slot_rows, feature_count),
        ln_gain[:, 0],
        ln_bias[:, 0],
        shard_count,
        group_size,
    )
    pieces = stream.shape[0]
    by_piece = labels.reshape(group_size * pieces, local_rows // pieces)
    residual, normed_mlp = exchange_call(
        attention_kernel,
        group_size,
        (
            normed,
            stream,
            w_attention,
            b_qkv[0][:, None, :],
            by_piece[:, :, None],
            by_piece[:, None, :],
            b_o,
            ln_gain[:, 1],
            ln_bias[:, 1],
        ),
        (
            jax.ShapeDtypeStruct(stream.shape, f32),
            jax.ShapeDtypeStruct(stream.shape, jnp.bfloat16),
        ),
        w_attention.shape[2],
        1,
        "attention",
    )
    stream = exchange_call(
        mlp_kernel,
        group_size,
        (normed_mlp, residual, w_up_full, b_up, w_down_rows, b_down),
        jax.ShapeDtypeStruct(stream.shape, jnp.bfloat16),
        w_up_full.shape[1],
        2,
        "mlp",
    ).reshape(local_rows, column_count)
    own_labels = lax.dynamic_slice_in_dim(labels, mp_index * local_rows, local_rows)
    return jnp.where(own_labels[:, None] >= 0, stream, jnp.zeros_like(stream))


def solution(mesh):
    in_specs = (
        P(("dp", "mp"), None, None),
        P(),
        P(("dp", "mp"), None),
        P(),
        P(),
        P(),
        P(),
        P(None, None, "dp", "mp"),
        P(None, None, "mp"),
        P(None, "mp", "dp"),
        P(),
        P(None, "dp", "mp"),
        P(None, "mp"),
        P(None, "mp", "dp"),
        P(),
    )
    out_specs = P(("dp", "mp"), None)
    return jax.shard_map(
        per_device, mesh=mesh, in_specs=in_specs, out_specs=out_specs, check_vma=False
    )
```

profile of v0, /device:TPU:0, one launch (start us, length us, event | category | flops | bytes accessed | tf_op | source)
XLA Modules:
  0.0 218.6 jit_solution(1761831950543724130)
XLA Ops:
  6.5 2.0 pad_maximum_fusion
  8.5 0.0 all-gather.4.cloned.1.call-update
  8.6 0.0 all-gather.6.cloned.1.call-start
  8.6 3.6 %fusion.5 = f32[8,64,1280]{2,1,0:T(8,128)S(1)} fusion(bf16[8,256,1280]{2,1,0:T(8,128)(2,1)} %param.15, s32[8,64]{1,0:T(8,128)} %param.17), kind=kOutput, calls=%fused_computation.10 | convolution fusion | flops 335675392 | bytes 7866368 | tf_op jit(solution)/shard_map/ijp,ipd->ijd/dot_general | solution.py:515
  12.2 0.6 fusion.2
  12.8 0.0 all-gather.6.cloned.1.call-update
  12.8 1.8 all_to_all.14
  14.6 2.5 %copy.24 = bf16[512,4,320]{0,2,1:T(8,128)(2,1)} copy(bf16[512,4,320]{2,1,0:T(4,128)(2,1)S(1)} %all_to_all.14) | data formatting | bytes 2621440 | tf_op jit(solution)/shard_map/all_to_all | solution.py:538
  17.0 5.3 %all-to-all-start = ((bf16[512,4,320]{0,2,1:T(8,128)(2,1)}), bf16[512,4,320]{0,2,1:T(8,128)(2,1)S(1)}, u32[]{:S(2)}, u32[]{:S(2)}) async-start(bf16[512,4,320]{0,2,1:T(8,128)(2,1)} %copy.24), calls=%async_computation | async-start | bytes 2621440 | tf_op jit(solution)/shard_map/all_to_all | solution.py:538
  22.4 0.5 select_reduce_fusion
  22.9 0.5 sub.30.label_col_ref
  23.4 0.1 sub.29.label_row_ref
  23.5 0.1 dynamic_slice.10
  23.5 0.1 subtract_subtract_fusion
  23.6 0.1 add_select_fusion
  23.7 0.1 select_n.36
  23.8 0.1 dynamic-slice_compare_fusion
  23.9 0.6 slice_bitcast_fusion
  24.5 14.4 %all-to-all-done = bf16[512,4,320]{0,2,1:T(8,128)(2,1)S(1)} async-done(((bf16[512,4,320]{0,2,1:T(8,128)(2,1)}), bf16[512,4,320]{0,2,1:T(8,128)(2,1)S(1)}, u32[]{:S(2)}, u32[]{:S(2)}) %all-to-all-start) | async-done | bytes 1310752 | tf_op jit(solution)/shard_map/all_to_all | solution.py:538
  38.8 1.3 copy.28
  40.2 3.5 %fusion.3 = bf16[1280,320]{0,1:T(8,128)(2,1)S(1)} fusion(bf16[2048,320]{0,1:T(8,128)(2,1)} %bitcast.31, s32[2048]{0:T(1024)S(1)} %select_n.36), kind=kOutput, calls=%fused_computation.5 | convolution fusion | flops 1680752640 | bytes 2138112 | tf_op jit(solution)/shard_map/dot_general | solution.py:547
  43.7 1.3 copy.26
  45.0 26.8 %route.1 = (bf16[2,160,1280]{2,1,0:T(8,128)(2,1)}, bf16[2,160,1280]{2,1,0:T(8,128)(2,1)}) custom-call(bf16[8,160,320]{2,1,0:T(8,128)(2,1)} %bitcast.32, f32[1,1280]{1,0:T(1,128)} %get-tuple-element.25.gain_ref, f32[1,1280]{1,0:T(1,128)} %get-tuple-element.22.shift_ref), custom_call_target="tpu_custom_call" | custom-call | flops 15000000512 | tf_op jit(solution)/shard_map/route/pallas_call | solution.py:141
  71.9 0.0 all-gather.4.cloned.1.call-done.w_ref
  71.9 1.1 copy-done.5
  73.1 1.1 copy-done.6
  74.2 70.5 %attention.1 = (f32[2,160,1280]{2,1,0:T(8,128)S(1)}, bf16[2,160,1280]{2,1,0:T(8,128)(2,1)S(1)}) custom-call(bf16[2,160,1280]{2,1,0:T(8,128)(2,1)S(1)} %copy-done.6, bf16[2,160,1280]{2,1,0:T(8,128)(2,1)S(1)} %copy-done.5, bf16[4,1280,320]{2,1,0:T(8,128)(2,1)} %all-gather.4.cloned.1.call-done.w_ref, f32[3,1,320]{2,1,0:T(1,128)S(1)} %bitcast.29, ...), custom_call_target="tpu_custom_call" | custom-call | flops 49999998976 | tf_op jit(solution)/shard_map/attention/pallas_call | solution.py:455
  144.8 0.9 copy-done.7
  145.6 3.0 %all-gather.8.cloned.1.call-done = bf16[1280,1280]{0,1:T(8,128)(2,1)} async-done(((bf16[1280,160]{0,1:T(8,128)(2,1)}), bf16[1280,1280]{0,1:T(8,128)(2,1)}) %all-gather.8.cloned.1.call-update) | async-done | bytes 3276816 | tf_op jit(solution)/shard_map/all_gather | solution.py:542
  148.6 1.1 copy-done.8
  149.7 61.2 %mlp.1 = bf16[2,160,1280]{2,1,0:T(8,128)(2,1)S(1)} custom-call(bf16[2,160,1280]{2,1,0:T(8,128)(2,1)S(1)} %copy-done.8, f32[2,160,1280]{2,1,0:T(8,128)S(1)} %get-tuple-element.18.residual_ref, bf16[1280,1280]{1,0:T(8,128)(2,1)} %all-gather.6.cloned.1.call-done.up_ref, f32[1,1280]{1,0:T(1,128)S(1)} %copy-done.2, bf16[1280,1280]{1,0:T(8,128)(2,1)} %bitcast.37, ...), custom_call_target="tpu_custom_call" | custom-call | flops 49999998976 | tf_op jit(solution)/shard_map/mlp/pallas_call | solution.py:455
  211.0 1.1 bitcast_select_fusion
  (32 shorter events, 0.1 us)
Async XLA Ops:
  6.5 5.6 %copy-start = (bf16[256,1280]{1,0:T(8,128)(2,1)S(1)}, bf16[256,1280]{1,0:T(8,128)(2,1)}, u32[]{:S(2)}) copy-start(bf16[256,1280]{1,0:T(8,128)(2,1)} %param.16) | copy-start | bytes 1966084
  6.5 65.3 %all-gather.4.cloned.1.call-start = ((), (), s32[]{:S(2)}) async-start(), calls=%async_computation.1 | async-start | bytes 4423680 | tf_op jit(solution)/shard_map/all_gather | solution.py:511
  8.5 3.7 %copy-start.9 = (s32[8,64]{1,0:T(8,128)S(1)}, s32[8,64]{1,0:T(8,128)}, u32[]{:S(2)}) copy-start(s32[8,64]{1,0:T(8,128)} %param.17) | copy-start | bytes 6148
  8.6 137.1 %all-gather.6.cloned.1.call-start = ((), (), s32[]{:S(2)}) async-start(), calls=%async_computation.2 | async-start | bytes 3686400 | tf_op jit(solution)/shard_map/all_gather | solution.py:519
  17.0 5.3 %copy-start.12 = (s32[256]{0:T(256)S(1)}, s32[256]{0:T(256)}, u32[]{:S(2)}) copy-start(s32[256]{0:T(256)} %param.19) | copy-start | bytes 3076
  17.0 5.3 %copy-start.13 = (s32[256]{0:T(256)S(1)}, s32[256]{0:T(256)}, u32[]{:S(2)}) copy-start(s32[256]{0:T(256)} %param.18) | copy-start | bytes 3076
  17.0 6.8 %copy-start.10 = (f32[1,2,1280]{2,1,0:T(2,128)S(1)}, f32[1,2,1280]{2,1,0:T(2,128)}, u32[]{:S(2)}) copy-start(f32[1,2,1280]{2,1,0:T(2,128)} %param.21) | copy-start | bytes 30724
  17.0 6.8 %copy-start.11 = (f32[1,2,1280]{2,1,0:T(2,128)S(1)}, f32[1,2,1280]{2,1,0:T(2,128)}, u32[]{:S(2)}) copy-start(f32[1,2,1280]{2,1,0:T(2,128)} %param.20) | copy-start | bytes 30724
  17.0 21.8 %all-to-all-start = ((bf16[512,4,320]{0,2,1:T(8,128)(2,1)}), bf16[512,4,320]{0,2,1:T(8,128)(2,1)S(1)}, u32[]{:S(2)}, u32[]{:S(2)}) async-start(bf16[512,4,320]{0,2,1:T(8,128)(2,1)} %copy.24), calls=%async_computation | async-start | bytes 2621440 | tf_op jit(solution)/shard_map/all_to_all | solution.py:538
  22.4 126.2 %all-gather.8.cloned.1.call-start = ((), (), s32[]{:S(2)}) async-start(), calls=%async_computation.3 | async-start | bytes 3686400 | tf_op jit(solution)/shard_map/all_gather | solution.py:542
  45.0 26.9 %copy-start.1 = (f32[1,1280]{1,0:T(1,128)S(1)}, f32[1,1280]{1,0:T(1,128)}, u32[]{:S(2)}) copy-start(f32[1,1280]{1,0:T(1,128)} %bias_ref.2) | copy-start | bytes 15364
  45.0 26.9 %copy-start.4 = (f32[1,3,320]{2,0,1:T(1,128)S(1)}, f32[1,3,320]{2,0,1:T(1,128)}, u32[]{:S(2)}) copy-start(f32[1,3,320]{2,0,1:T(1,128)} %param.23) | copy-start | bytes 11524
  71.9 1.1 copy-start.5
  73.1 1.1 copy-start.6
  74.2 74.4 %copy-start.2 = (f32[1,1280]{1,0:T(1,128)S(1)}, f32[1,1280]{1,0:T(1,128)}, u32[]{:S(2)}) copy-start(f32[1,1280]{1,0:T(1,128)} %b_ref.1) | copy-start | bytes 15364
  74.2 74.4 %copy-start.3 = (f32[1,1280]{1,0:T(1,128)S(1)}, f32[1,1280]{1,0:T(1,128)}, u32[]{:S(2)}) copy-start(f32[1,1280]{1,0:T(1,128)} %bias_ref.3) | copy-start | bytes 15364
  144.7 0.9 copy-start.7
  148.6 1.1 copy-start.8
Sparse Core Ops, SparseCore 0:
  8.9 56.6 all-gather.3
  67.3 40.7 all-gather.5
  109.8 38.7 all-gather.7
where the time goes:
time: 219 us
  Pallas kernels  159 us (73%)
  waiting for transfers between devices  17.4 us (8%)
  between operations  13.3 us (6%)
  local copies, waits for them, and re-layouts  12.5 us (6%)
  matrix products  7.64 us (3%)
  starting transfers between devices  5.38 us (2%)
  other arithmetic  3.75 us (2%)
    pallas_call x2, Pallas kernels, exchange_call(): pl.pallas_call(functools.partial(kernel, groups), out_shape=outs, in_spec...  132 us
    pallas_call x1, Pallas kernels, route(): pl.pallas_call(functools.partial(route_kernel, shards, groups), out_shape...  26.8 us
    all_to_all x1, waiting for transfers between devices, per_device(): lax.all_to_all(tokens.reshape(-1, column_count), 'mp', split_axis=1, conc...  14.4 us
    all_to_all x3, local copies, waits for them, and re-layouts, per_device(): lax.all_to_all(tokens.reshape(-1, column_count), 'mp', split_axis=1, conc...  5.57 us
    all_to_all x1, starting transfers between devices, per_device(): lax.all_to_all(tokens.reshape(-1, column_count), 'mp', split_axis=1, conc...  5.33 us
  transfers between devices with their start and end apart: 4, of which 2 were waited for; matrix products, arithmetic and copies ran while one was open for 7% of the time, Pallas kernels for 45%

commit v1 on v0

--- a/solution.py
+++ b/solution.py
@@ -476,6 +476,10 @@
         name=name,
     )(*args)
 
+def slot_size(images_here, shards, keep_most):
+    per_slot = (images_here + shards - 1) // shards
+    return max(keep_most + 16, per_slot * keep_most * 5 // 8)
+
 
 def per_device(
     patches,
@@ -499,8 +503,7 @@
     shard_count = lax.axis_size("dp")
     group_size = lax.axis_size("mp")
     images_here = local_images * group_size
-    per_slot = (images_here + shard_count - 1) // shard_count
-    slot_rows = max(keep_most + 16, per_slot * keep_most * 5 // 8)
+    slot_rows = slot_size(images_here, shard_count, keep_most)
     pack_rows = slot_rows * shard_count
     local_rows = pack_rows // group_size
     dp_index = lax.axis_index("dp")
@@ -588,6 +591,838 @@
     own_labels = lax.dynamic_slice_in_dim(labels, mp_index * local_rows, local_rows)
     return jnp.where(own_labels[:, None] >= 0, stream, jnp.zeros_like(stream))
 
+def by_pair(index, values):
+    low = index % 2
+    high = index // 2
+    return (
+        values[0] * (1 - low) * (1 - high)
+        + values[1] * low * (1 - high)
+        + values[2] * (1 - low) * high
+        + values[3] * low * high
+    )
+
+
+ARRIVALS = ((0, 1, 2, 3), (1, 0, 2, 3), (2, 1, 3, 0), (3, 2, 1, 0))
+
+
+def layer_kernel(
+    shards,
+    groups,
+    patches_ref,
+    position_ref,
+    keep_ref,
+    target_ref,
+    label_col_ref,
+    label_row_ref,
+    gain_ref,
+    shift_ref,
+    attention_shard_ref,
+    b_attention_ref,
+    b_o_ref,
+    mlp_shard_ref,
+    b_up_ref,
+    b_down_ref,
+    out_ref,
+    patch_buf,
+    token_out,
+    token_in,
+    slot_out,
+    slot_in,
+    w_attention,
+    b_attention,
+    w_mlp,
+    normed_ref,
+    projected_ref,
+    attended_ref,
+    residual_ref,
+    blocks,
+    parts,
+    backs,
+    relay,
+    hidden_ref,
+    patch_sem,
+    local_sem,
+    token_send,
+    token_recv,
+    slot_send,
+    slot_recv,
+    bias_send,
+    bias_recv,
+    att_up,
+    att_down,
+    att_plane,
+    att_twin,
+    att_recv,
+    att_twin_recv,
+    mlp_up,
+    mlp_down,
+    mlp_twin,
+    mlp_recv,
+    mlp_twin_recv,
+    send_a,
+    recv_a,
+    send_b,
+    recv_b,
+):
+    f32 = jnp.float32
+    bf16 = jnp.bfloat16
+    dp = lax.axis_index("dp")
+    mp = lax.axis_index("mp")
+    per = shards // groups
+    planes = shards // 2
+    z = dp // 2
+    core = dp % 2
+    home = dp // per
+    images, patch_count, depth = patches_ref.shape
+    keep_most = keep_ref.shape[1]
+    feature = depth // groups
+    pieces, piece_rows = blocks.shape[1:3]
+    shard_rows = attention_shard_ref.shape[0]
+    half_images = images // 2
+    last = planes - 1
+
+    def remote(source, target, out_sem, in_sem, device):
+        return pltpu.make_async_remote_copy(
+            src_ref=source,
+            dst_ref=target,
+            send_sem=out_sem,
+            recv_sem=in_sem,
+            device_id=device,
+            device_id_type=MESH,
+        )
+
+    def peer(k):
+        return (dp, flip(mp, k, groups))
+
+    twin = (dp + 1 - 2 * core, mp)
+    above = (lax.rem(dp + 2, shards), mp)
+    below = (lax.rem(dp + shards - 2, shards), mp)
+
+    for i in range(images):
+        pltpu.make_async_copy(patches_ref.at[i], patch_buf.at[i], patch_sem.at[i]).start()
+
+    barrier = pltpu.get_barrier_semaphore()
+    for j in range(per):
+        for g in range(groups):
+            source = mp * per + j
+
+            @pl.when(jnp.logical_or(source != dp, mp != g))
+            def _():
+                pl.semaphore_signal(barrier, inc=1, device_id=(source, g), device_id_type=MESH)
+
+    for k in range(1, groups):
+        pl.semaphore_signal(barrier, inc=1, device_id=peer(k), device_id_type=MESH)
+    pl.semaphore_signal(barrier, inc=1, device_id=twin, device_id_type=MESH)
+
+    @pl.when(z < last)
+    def _():
+        pl.semaphore_signal(barrier, inc=1, device_id=above, device_id_type=MESH)
+
+    @pl.when(z > 0)
+    def _():
+        pl.semaphore_signal(barrier, inc=1, device_id=below, device_id_type=MESH)
+
+    own_rows = pl.ds(pl.multiple_of(dp * shard_rows, 16), shard_rows)
+    own_att = pltpu.make_async_copy(
+        attention_shard_ref, w_attention.at[mp, own_rows, :], local_sem.at[0]
+    )
+    own_mlp = pltpu.make_async_copy(mlp_shard_ref, w_mlp.at[:, own_rows, :], local_sem.at[1])
+    own_bias = pltpu.make_async_copy(b_attention_ref, b_attention.at[mp], local_sem.at[2])
+    own_att.start()
+    own_mlp.start()
+    own_bias.start()
+    is_home = home == mp
+    away = jnp.where(is_home, 0, 1)
+    between = jnp.where(jnp.logical_and(z > 0, z < last), 1, 0)
+    pl.semaphore_wait(barrier, shards + groups + away + between)
+
+    own_att.wait()
+    own_mlp.wait()
+    own_bias.wait()
+
+    def rows_of(plane):
+        return pl.ds(pl.multiple_of((2 * plane + core) * shard_rows, 16), shard_rows)
+
+    def att_copy(group, plane, out_sem, device):
+        at = w_attention.at[group, rows_of(plane), :]
+        return remote(at, at, out_sem, att_recv.at[group * planes + plane], device)
+
+    def att_to_twin(group, plane):
+        at = w_attention.at[group, rows_of(plane), :]
+        index = group * planes + plane
+        return remote(at, at, att_twin.at[index], att_twin_recv.at[index], twin)
+
+    def att_over(k, group, plane, relayed):
+        return att_copy(group, plane, att_plane.at[(k * 2 + relayed) * planes + plane], peer(k))
+
+    def arrival(p):
+        return by_pair(z, [row[p] for row in ARRIVALS])
+
+    def att_held(p):
+        plane = arrival(p)
+        if p > 0:
+            att_copy(mp, plane, att_up.at[plane], twin).wait_recv()
+
+        @pl.when(jnp.logical_and(plane <= z, z < last))
+        def _():
+            att_copy(mp, plane, att_up.at[plane], above).start()
+
+        @pl.when(jnp.logical_and(plane >= z, z > 0))
+        def _():
+            att_copy(mp, plane, att_down.at[plane], below).start()
+
+        att_to_twin(mp, plane).start()
+
+    def att_spread(p):
+        plane = arrival(p)
+        for k in (1, 2):
+            att_over(k, mp, plane, 0).start()
+
+    def att_near(p):
+        plane = arrival(p)
+        for k in (1, 2):
+            group = flip(mp, k, groups)
+            att_copy(group, plane, att_up.at[plane], twin).wait_recv()
+            if p % 2 == k - 1:
+                att_over(3 - k, group, plane, 1).start()
+            att_to_twin(group, plane).start()
+
+    def att_far(p):
+        plane = arrival(p)
+        group = flip(mp, 3, groups)
+        att_copy(group, plane, att_up.at[plane], twin).wait_recv()
+        att_to_twin(group, plane).start()
+
+    def mlp_copy(j, plane, out_sem, device):
+        at = w_mlp.at[j, rows_of(plane), :]
+        return remote(at, at, out_sem, mlp_recv.at[j * planes + plane], device)
+
+    def mlp_to_twin(j, plane):
+        at = w_mlp.at[j, rows_of(plane), :]
+        index = j * planes + plane
+        return remote(at, at, mlp_twin.at[index], mlp_twin_recv.at[index], twin)
+
+    def mlp_held(j, p):
+        plane = arrival(p)
+        index = j * planes + plane
+        if p > 0:
+            mlp_copy(j, plane, mlp_up.at[index], twin).wait_recv()
+
+        @pl.when(jnp.logical_and(plane <= z, z < last))
+        def _():
+            mlp_copy(j, plane, mlp_up.at[index], above).start()
+
+        @pl.when(jnp.logical_and(plane >= z, z > 0))
+        def _():
+            mlp_copy(j, plane, mlp_down.at[index], below).start()
+
+        mlp_to_twin(j, plane).start()
+
+    def bias_copy(k):
+        return remote(
+            b_attention.at[mp], b_attention.at[mp], bias_send.at[k], bias_recv.at[mp], peer(k)
+        )
+
+    for k in range(1, groups):
+        bias_copy(k).start()
+    att_held(0)
+
+    def token_copy(g, i):
+        rows = pl.ds(pl.multiple_of(i * keep_most, keep_most), keep_most)
+        return remote(
+            token_out.at[g, rows, :],
+            token_in.at[mp, rows, :],
+            token_send.at[g * half_images + i],
+            token_recv.at[mp * half_images + i],
+            (dp, g),
+        )
+
+    def own_tokens(i):
+        rows = pl.ds(pl.multiple_of(i * keep_most, keep_most), keep_most)
+        return pltpu.make_async_copy(
+            token_out.at[mp, rows, :],
+            token_in.at[mp, rows, :],
+            token_recv.at[mp * half_images + i],
+        )
+
+    patch_ids = lax.broadcasted_iota(jnp.int32, (keep_most, patch_count), 1)
+
+    def pick(i):
+        pltpu.make_async_copy(patches_ref.at[i], patch_buf.at[i], patch_sem.at[i]).wait()
+        chosen = (keep_ref[i] == patch_ids).astype(bf16)
+        return jnp.dot(chosen, patch_buf[i], preferred_element_type=f32) + jnp.dot(
+            chosen, position_ref[...], preferred_element_type=f32
+        )
+
+    def some_tokens(i, carry):
+        rows = pl.ds(pl.multiple_of(i * keep_most, keep_most), keep_most)
+        left = pick(i)
+        right = pick(i + half_images)
+        for g in range(groups):
+            at = slice(g * feature, (g + 1) * feature)
+            token_out[g, rows, :] = jnp.concatenate([left[:, at], right[:, at]], axis=-1).astype(
+                bf16
+            )
+        for g in range(groups):
+
+            @pl.when(mp != g)
+            def _():
+                token_copy(g, i).start()
+
+        own_tokens(i).start()
+        return carry
+
+    lax.fori_loop(0, half_images, some_tokens, 0)
+    att_spread(0)
+    att_held(1)
+    att_spread(1)
+
+    def tokens_here(k, carry):
+        group = flip(mp, k, groups)
+
+        def one(i, carry):
+            remote(
+                token_out.at[0, pl.ds(0, keep_most), :],
+                token_in.at[group, pl.ds(pl.multiple_of(i * keep_most, keep_most), keep_most), :],
+                token_send.at[0],
+                token_recv.at[group * half_images + i],
+                twin,
+            ).wait_recv()
+            return carry
+
+        return lax.fori_loop(0, half_images, one, carry)
+
+    for i in range(half_images):
+        own_tokens(i).wait()
+    lax.fori_loop(1, groups, tokens_here, 0)
+
+    def slot_copy(dest):
+        slot = lax.rem(dp, per) * groups + mp
+        return remote(
+            slot_out.at[dest],
+            slot_in.at[slot],
+            slot_send.at[dest],
+            slot_recv.at[slot],
+            (dest, home),
+        )
+
+    def own_slot():
+        slot = lax.rem(dp, per) * groups + mp
+        return pltpu.make_async_copy(slot_out.at[dp], slot_in.at[slot], slot_recv.at[slot])
+
+    slot_rows = 2 * slot_out.shape[1]
+    half_rows = slot_out.shape[1]
+    token_count = groups * half_images * keep_most
+    edge = feature // 128 * 128
+    width = feature - edge + feature
+
+    def place(i, carry):
+        first = 2 * i * slot_rows
+        rows = first + lax.broadcasted_iota(jnp.int32, (2 * slot_rows, token_count), 0)
+        left = (rows == target_ref[0]).astype(bf16)
+        right = (rows == target_ref[1]).astype(bf16)
+        tokens = token_in[...].reshape(token_count, 2 * feature)
+        whole = (
+            jnp.dot(left, tokens[:, :width], preferred_element_type=f32)[:, :feature]
+            + jnp.dot(right, tokens[:, edge:], preferred_element_type=f32)[:, feature - edge :]
+        )
+        for j in range(2):
+            upper = whole[2 * j * half_rows : (2 * j + 1) * half_rows]
+            lower = whole[(2 * j + 1) * half_rows : (2 * j + 2) * half_rows]
+            slot_out[2 * i + j] = jnp.concatenate([upper, lower], axis=-1).astype(bf16)
+        for j in range(2):
+            dest = 2 * i + j
+            stays = jnp.logical_and(is_home, dest == dp)
+
+            @pl.when(stays)
+            def _():
+                own_slot().start()
+
+            @pl.when(jnp.logical_not(stays))
+            def _():
+                slot_copy(dest).start()
+
+        return carry
+
+    lax.fori_loop(0, shards // 2, place, 0)
+    att_held(2)
+    att_spread(2)
+    att_near(0)
+    att_held(3)
+    att_spread(3)
+    mlp_held(0, 0)
+
+    for j in range(per):
+        for g in range(groups):
+            source = mp * per + j
+            stays = jnp.logical_and(source == dp, mp == g)
+
+            @pl.when(stays)
+            def _():
+                own_slot().wait()
+
+            @pl.when(jnp.logical_not(stays))
+            def _():
+                remote(
+                    slot_out.at[0],
+                    slot_in.at[j * groups + g],
+                    slot_send.at[0],
+                    slot_recv.at[j * groups + g],
+                    twin,
+                ).wait_recv()
+
+    rows_tile = tile_of(half_rows, 16)
+    steps = half_rows // rows_tile
+
+    def assemble(i, carry):
+        j = i // (2 * steps)
+        half = (i // steps) % 2
+        rows = pl.ds(pl.multiple_of((i % steps) * rows_tile, rows_tile), rows_tile)
+
+        def put(low):
+            whole = jnp.concatenate(
+                [
+                    slot_in[j * groups + g, rows, :].astype(f32)[:, low : low + feature]
+                    for g in range(groups)
+                ],
+                axis=-1,
+            )
+            to = pl.ds(pl.multiple_of(i * rows_tile, rows_tile), rows_tile)
+            residual_ref[to, :] = whole + b_o_ref[...]
+            normed_ref[to, :] = norm_rows(whole, gain_ref[0:1], shift_ref[0:1])
+
+        @pl.when(half == 0)
+        def _():
+            put(0)
+
+        @pl.when(half == 1)
+        def _():
+            put(feature)
+
+        return carry
+
+    lax.fori_loop(0, 2 * per * steps, assemble, 0)
+    mlp_held(0, 1)
+
+    heads = feature // HEAD
+    scale = 1.0 / math.sqrt(HEAD)
+    used = 3 * feature
+    total_width = w_attention.shape[2]
+    column = 256
+    low_out = used // 128 * 128
+    low_key = feature // 128 * 128
+
+    def one_group(step, carry):
+        group = flip(mp, step, groups)
+
+        @pl.when(step == 1)
+        def _():
+            mlp_held(0, 2)
+            for p in range(1, planes):
+                att_near(p)
+            mlp_held(0, 3)
+            mlp_held(1, 0)
+            att_far(0)
+            att_far(1)
+
+        @pl.when(step == 2)
+        def _():
+            mlp_held(1, 1)
+
+        @pl.when(step == 3)
+        def _():
+            att_far(2)
+            att_far(3)
+            mlp_held(1, 2)
+
+        @pl.when(step > 0)
+        def _():
+            remote(
+                b_attention.at[0], b_attention.at[group], bias_send.at[0], bias_recv.at[group], twin
+            ).wait_recv()
+
+        for plane in range(planes):
+            at = w_attention.at[group, pl.ds(0, shard_rows), :]
+            remote(
+                at, at, att_twin.at[0], att_twin_recv.at[group * planes + plane], twin
+            ).wait_recv()
+
+        def project(t, carry):
+            at = pl.ds(pl.multiple_of(t * column, column), column)
+            y = jnp.dot(normed_ref[...], w_attention[group, :, at], preferred_element_type=f32)
+            projected_ref[:, at] = (y + b_attention[group, 0:1, at]).astype(bf16)
+            return carry
+
+        lax.fori_loop(0, projected_ref.shape[1] // column, project, 0)
+
+        def one_slot(j, carry):
+            rows = pl.ds(pl.multiple_of(j * slot_rows, 16), slot_rows)
+            query = projected_ref[rows, 0:feature]
+            key = projected_ref[rows, low_key : 2 * feature].astype(f32)[:, feature - low_key :]
+            key = key.astype(bf16)
+            value = projected_ref[rows, 2 * feature : used]
+            matches = label_col_ref[j] == label_row_ref[j]
+            spans = [(t, min(t + 128, feature)) for t in range(0, feature, 128)]
+            totals = [jnp.zeros((slot_rows, high - low), f32) for low, high in spans]
+            for h in range(heads):
+                low = h * HEAD // 128 * 128
+                high = min(((h + 1) * HEAD + 127) // 128 * 128, feature)
+                lane = low + lax.broadcasted_iota(jnp.int32, (slot_rows, high - low), 1)
+                inside = (lane >= h * HEAD) & (lane < (h + 1) * HEAD)
+                zero = jnp.zeros((slot_rows, high - low), bf16)
+                scores = lax.dot_general(
+                    jnp.where(inside, query[:, low:high], zero),
+                    key[:, low:high],
+                    (((1,), (1,)), ((), ())),
+                    preferred_element_type=f32,
+                )
+                scores = jnp.where(matches, scores * scale, -jnp.inf)
+                weights = jnp.exp(scores - jnp.max(scores, axis=-1, keepdims=True))
+                inverse = 1.0 / jnp.sum(weights, axis=-1, keepdims=True)
+                probabilities = (weights * inverse).astype(bf16)
+                y = jnp.dot(
+                    probabilities,
+                    jnp.where(inside, value[:, low:high], zero),
+                    preferred_element_type=f32,
+                )
+                for s, (a, b) in enumerate(spans):
+                    if low <= a and b <= high:
+                        totals[s] = totals[s] + y[:, a - low : b - low]
+            shifted = jnp.concatenate(
+                [jnp.zeros((slot_rows, used - low_out), f32)] + totals, axis=-1
+            )
+            attended_ref[rows, :] = shifted.astype(bf16)
+            return carry
+
+        lax.fori_loop(0, per, one_slot, 0)
+
+        def out_column(t, carry):
+            at = pl.ds(pl.multiple_of(t * column, column), column)
+            residual_ref[:, at] = residual_ref[:, at] + lax.dot_general(
+                attended_ref[...],
+                w_attention[group, at, low_out:total_width],
+                (((1,), (1,)), ((), ())),
+                preferred_element_type=f32,
+            )
+            return carry
+
+        lax.fori_loop(0, depth // column, out_column, 0)
+        return carry
+
+    lax.fori_loop(0, groups, one_group, 0)
+
+    norm_tile = tile_of(piece_rows, 32)
+    for h in range(pieces):
+
+        def norm_some(i, carry, h=h):
+            rows = pl.ds(pl.multiple_of(i * norm_tile, norm_tile), norm_tile)
+            at = pl.ds(pl.multiple_of(h * piece_rows + i * norm_tile, norm_tile), norm_tile)
+            blocks[0, h, rows, :] = norm_rows(residual_ref[at, :], gain_ref[1:2], shift_ref[1:2])
+            return carry
+
+        lax.fori_loop(0, piece_rows // norm_tile, norm_some, 0)
+
+    def out_copy(k, h):
+        at = k * pieces + h
+        return remote(blocks.at[0, h], blocks.at[k, h], send_a.at[at], recv_a.at[at], peer(k))
+
+    def back_copy(k, h):
+        at = k * pieces + h
+        return remote(parts.at[k, h], backs.at[k, h], send_b.at[at], recv_b.at[at], peer(k))
+
+    def forward(h):
+        held, k = (1, 2) if h == 0 else (2, 1)
+        at = 3 * pieces + h
+        return remote(blocks.at[held, h], blocks.at[3, h], send_a.at[at], recv_a.at[at], peer(k))
+
+    def across(h):
+        at = 3 * pieces + h
+        return remote(parts.at[3, h], relay.at[h], send_b.at[at], recv_b.at[at], peer(1 + h))
+
+    for k, h in ((1, 0), (2, 1), (1, 1), (2, 0)):
+        out_copy(k, h).start()
+    mlp_held(1, 3)
+    for j in range(2):
+        for plane in range(planes):
+            at = w_mlp.at[0, pl.ds(0, shard_rows), :]
+            remote(
+                at, at, mlp_twin.at[0], mlp_twin_recv.at[j * planes + plane], twin
+            ).wait_recv()
+
+    def mlp_step(i, carry):
+        late = (i + 2) // 8
+        middle = ((i + 2) // 4) % 2
+        k = middle * (1 + i % 2) + 3 * late
+        h = (i // 4 + i % 2) % 2
+
+        @pl.when(i == 2)
+        def _():
+            out_copy(1, 0).wait_recv()
+            forward(0).start()
+            out_copy(2, 1).wait_recv()
+            forward(1).start()
+
+        @pl.when(i >= 4)
+        def _():
+            out_copy(k, h).wait_recv()
+
+        def up(t, carry):
+            at = pl.ds(pl.multiple_of(t * column, column), column)
+            y = jnp.dot(blocks[k, h], w_mlp[0, :, at], preferred_element_type=f32) + b_up_ref[:, at]
+            y = 0.5 * y * (1.0 + lax.erf(y * math.sqrt(0.5)))
+            hidden_ref[:, at] = y.astype(bf16)
+            return carry
+
+        lax.fori_loop(0, hidden_ref.shape[1] // column, up, 0)
+
+        def down(t, carry):
+            at = pl.ds(pl.multiple_of(t * column, column), column)
+            parts[k, h, :, at] = lax.dot_general(
+                hidden_ref[...],
+                w_mlp[1, at, :],
+                (((1,), (1,)), ((), ())),
+                preferred_element_type=f32,
+            ).astype(bf16)
+            return carry
+
+        lax.fori_loop(0, depth // column, down, 0)
+
+        @pl.when(i == 2)
+        def _():
+            back_copy(1, 0).start()
+
+        @pl.when(i == 3)
+        def _():
+            back_copy(2, 1).start()
+
+        @pl.when(i == 6)
+        def _():
+            across(1).start()
+
+        @pl.when(i == 7)
+        def _():
+            across(0).start()
+
+        return carry
+
+    lax.fori_loop(0, 8, mlp_step, 0)
+    for h, k in ((1, 1), (0, 2)):
+        across(h).wait_recv()
+
+        def add(i, carry, h=h, k=k):
+            rows = pl.ds(pl.multiple_of(i * norm_tile, norm_tile), norm_tile)
+            parts[k, h, rows, :] = (
+                parts[k, h, rows, :].astype(f32) + relay[h, rows, :].astype(f32)
+            ).astype(bf16)
+            return carry
+
+        lax.fori_loop(0, piece_rows // norm_tile, add, 0)
+        back_copy(k, h).start()
+    for k, h in ((1, 0), (2, 1), (1, 1), (2, 0)):
+        back_copy(k, h).wait_recv()
+    for h in range(pieces):
+
+        def finish(i, carry, h=h):
+            rows = pl.ds(pl.multiple_of(i * norm_tile, norm_tile), norm_tile)
+            at = pl.ds(pl.multiple_of(h * piece_rows + i * norm_tile, norm_tile), norm_tile)
+            total = residual_ref[at, :] + b_down_ref[...] + parts[0, h, rows, :].astype(f32)
+            for k in (1, 2):
+                total = total + backs[k, h, rows, :].astype(f32)
+            live = label_col_ref[h, rows, :] >= 0
+            out_ref[h, rows, :] = jnp.where(live, total, 0.0).astype(bf16)
+            return carry
+
+        lax.fori_loop(0, piece_rows // norm_tile, finish, 0)
+
+    for h in range(2):
+        forward(h).wait_send()
+        across(h).wait_send()
+        for k in (1, 2):
+            out_copy(k, h).wait_send()
+            back_copy(k, h).wait_send()
+    for k in range(1, groups):
+        bias_copy(k).wait_send()
+    for g in range(groups):
+
+        @pl.when(mp != g)
+        def _():
+            for i in range(half_images):
+                token_copy(g, i).wait_send()
+
+    def slot_sent(dest, carry):
+        @pl.when(jnp.logical_not(jnp.logical_and(is_home, dest == dp)))
+        def _():
+            slot_copy(dest).wait_send()
+
+        return carry
+
+    lax.fori_loop(0, shards, slot_sent, 0)
+    for p in range(planes):
+        plane = arrival(p)
+
+        @pl.when(jnp.logical_and(plane <= z, z < last))
+        def _():
+            att_copy(mp, plane, att_up.at[plane], above).wait_send()
+            for j in range(2):
+                mlp_copy(j, plane, mlp_up.at[j * planes + plane], above).wait_send()
+
+        @pl.when(jnp.logical_and(plane >= z, z > 0))
+        def _():
+            att_copy(mp, plane, att_down.at[plane], below).wait_send()
+            for j in range(2):
+                mlp_copy(j, plane, mlp_down.at[j * planes + plane], below).wait_send()
+
+        for g in range(groups):
+            att_to_twin(g, plane).wait_send()
+        for j in range(2):
+            mlp_to_twin(j, plane).wait_send()
+        for k in (1, 2):
+            att_over(k, mp, plane, 0).wait_send()
+        k = 1 + p % 2
+        att_over(3 - k, flip(mp, k, groups), plane, 1).wait_send()
+
+
+def layer_call(shards, groups, args, slot_rows):
+    patches, keep, attention_shard, mlp_shard = args[0], args[2], args[8], args[11]
+    images, _, depth = patches.shape
+    keep_most = keep.shape[1]
+    feature = depth // groups
+    per = shards // groups
+    rows = per * slot_rows
+    planes = shards // 2
+    half_images = images // 2
+    vmem = pl.BlockSpec(memory_space=pltpu.VMEM)
+    bf16 = jnp.bfloat16
+    hidden = mlp_shard.shape[2]
+    dma = pltpu.SemaphoreType.DMA
+    buffer = pltpu.VMEM((groups, per, slot_rows, depth), bf16)
+    used = 3 * feature
+    return pl.pallas_call(
+        functools.partial(layer_kernel, shards, groups),
+        out_shape=jax.ShapeDtypeStruct((per, slot_rows, depth), bf16),
+        in_specs=[pl.BlockSpec(memory_space=pl.ANY)] + [vmem] * (len(args) - 1),
+        out_specs=vmem,
+        scratch_shapes=[
+            pltpu.VMEM(patches.shape, bf16),
+            pltpu.VMEM((groups, half_images * keep_most, 2 * feature), bf16),
+            pltpu.VMEM((groups, half_images * keep_most, 2 * feature), bf16),
+            pltpu.VMEM((shards, slot_rows // 2, 2 * feature), bf16),
+            pltpu.VMEM((shards, slot_rows // 2, 2 * feature), bf16),
+            pltpu.VMEM((groups, shards * attention_shard.shape[0], attention_shard.shape[1]), bf16),
+            pltpu.VMEM((groups,) + args[9].shape, jnp.float32),
+            pltpu.VMEM((2, shards * mlp_shard.shape[1], hidden), bf16),
+            pltpu.VMEM((rows, depth), bf16),
+            pltpu.VMEM((rows, args[9].shape[1]), bf16),
+            pltpu.VMEM((rows, attention_shard.shape[1] - used // 128 * 128), bf16),
+            pltpu.VMEM((rows, depth), jnp.float32),
+            buffer,
+            buffer,
+            buffer,
+            pltpu.VMEM((per, slot_rows, depth), bf16),
+            pltpu.VMEM((slot_rows, hidden), bf16),
+            dma((images,)),
+            dma((3,)),
+            dma((groups * half_images,)),
+            dma((groups * half_images,)),
+            dma((shards,)),
+            dma((shards,)),
+            dma((groups,)),
+            dma((groups,)),
+            dma((planes,)),
+            dma((planes,)),
+            dma((6 * planes,)),
+            dma((groups * planes,)),
+            dma((groups * planes,)),
+            dma((groups * planes,)),
+            dma((2 * planes,)),
+            dma((2 * planes,)),
+            dma((2 * planes,)),
+            dma((2 * planes,)),
+            dma((2 * planes,)),
+            dma((groups * per,)),
+            dma((groups * per,)),
+            dma((groups * per,)),
+            dma((groups * per,)),
+        ],
+        compiler_params=pltpu.CompilerParams(
+            collective_id=3, has_side_effects=True, vmem_limit_bytes=60 * 1024 * 1024
+        ),
+        cost_estimate=pl.CostEstimate(flops=100_000_000_000, bytes_accessed=0, transcendentals=0),
+        name="layer",
+    )(*args)
+
+
+def one_kernel(
+    patches,
+    position,
+    keep,
+    counts,
+    offsets,
+    ln_gain,
+    ln_bias,
+    w_qkv,
+    b_qkv,
+    w_o,
+    b_o,
+    w_up,
+    b_up,
+    w_down,
+    b_down,
+):
+    local_images, _, depth = patches.shape
+    keep_most = keep.shape[1]
+    shards = lax.axis_size("dp")
+    groups = lax.axis_size("mp")
+    images_here = local_images * groups
+    slot_rows = slot_size(images_here, shards, keep_most)
+    pack_rows = slot_rows * shards
+    per = shards // groups
+    dp = lax.axis_index("dp")
+    mp = lax.axis_index("mp")
+    feature = depth // groups
+
+    own_counts = lax.dynamic_slice_in_dim(counts, dp * images_here, images_here)
+    own_offsets = lax.dynamic_slice_in_dim(offsets, dp * images_here, images_here)
+    shard = own_offsets // pack_rows
+    base = shard * slot_rows + own_offsets - shard * pack_rows - dp * slot_rows
+    step = jnp.arange(keep_most, dtype=jnp.int32)
+    target = jnp.where(step[None, :] < own_counts[:, None], base[:, None] + step[None, :], -1)
+    target = target.reshape(groups, 2, -1).transpose(1, 0, 2).reshape(2, 1, -1)
+
+    first = dp * pack_rows + mp * per * slot_rows
+    rows = first + jnp.arange(per * slot_rows, dtype=jnp.int32)
+    inside = (rows[:, None] >= offsets[None, :]) & (rows[:, None] < (offsets + counts)[None, :])
+    image_ids = jnp.arange(counts.shape[0], dtype=jnp.int32)
+    labels = jnp.max(jnp.where(inside, image_ids[None, :] + 1, 0), axis=1) - 1
+    labels = labels.reshape(per, slot_rows)
+
+    attention_shard = jnp.concatenate([w_qkv[0, 0], w_qkv[0, 1], w_qkv[0, 2], w_o[0].T], axis=1)
+    mlp_shard = jnp.stack([w_up[0], w_down[0].T])
+    bias = b_qkv[0].reshape(1, -1)
+    pad = (3 * feature + 255) // 256 * 256 - 3 * feature
+    bias = jnp.broadcast_to(jnp.pad(bias, ((0, 0), (0, pad))), (8, 3 * feature + pad))
+    return layer_call(
+        shards,
+        groups,
+        (
+            patches,
+            position,
+            keep[:, :, None],
+            target,
+            labels[:, :, None],
+            labels[:, None, :],
+            ln_gain[0],
+            ln_bias[0],
+            attention_shard,
+            bias,
+            b_o,
+            mlp_shard,
+            b_up,
+            b_down,
+        ),
+        slot_rows,
+    ).reshape(per * slot_rows, depth)
+
 
 def solution(mesh):
     in_specs = (
@@ -608,6 +1443,7 @@
         P(),
     )
     out_specs = P(("dp", "mp"), None)
+    square = mesh.shape["mp"] == 4 and mesh.shape["dp"] == 8
     return jax.shard_map(
-        per_device, mesh=mesh, in_specs=in_specs, out_specs=out_specs, check_vma=False
+        one_kernel if square else per_device, mesh=mesh, in_specs=in_specs, out_specs=out_specs, check_vma=False
     )

time: 219 us -> 199 us (0.909)
  Pallas kernels: 159 us -> 183 us
  waiting for transfers between devices: 17.4 us -> 0 us
  between operations: 13.3 us -> 0.03 us
  matrix products: 7.64 us -> 0 us
  starting transfers between devices: 5.38 us -> 0 us
    pallas_call x3 -> x1, Pallas kernels: 159 us -> 183 us  [layer_call(): pl.pallas_call(functools.partial(layer_kernel, shards, groups), out_shape...]
    all_to_all x1 -> x0, waiting for transfers between devices: 14.4 us -> none  [per_device(): lax.all_to_all(tokens.reshape(-1, column_count), 'mp', split_axis=1, conc...]
    dot_general x3 -> x0, matrix products: 7.64 us -> none  [the longest x1 3.57 us: per_device(): jnp.einsum('ijp,ipd->ijd', chosen, patches, preferred_element_type=f32)]
    all_to_all x3 -> x0, local copies, waits for them, and re-layouts: 5.57 us -> none  [per_device(): lax.all_to_all(tokens.reshape(-1, column_count), 'mp', split_axis=1, conc...]
    all_to_all x1 -> x0, starting transfers between devices: 5.33 us -> none  [per_device(): lax.all_to_all(tokens.reshape(-1, column_count), 'mp', split_axis=1, conc...]
    all_gather x3 -> x0, waiting for transfers between devices: 2.98 us -> none  [the longest x1 2.96 us: per_device(): w_down_rows = lax.all_gather(w_down_shard, 'dp', axis=1, tiled=True).T]
    unnamed x28 -> x1, local copies, waits for them, and re-layouts: 4.36 us -> 2.09 us
  transfers between devices with their start and end apart: 4 -> 0, of which waited for: 2 -> 0; matrix products, arithmetic and copies ran while one was open for 7% -> 0% of each run, Pallas kernels for 45% -> 0%
where the time goes in v1:
time: 199 us
  Pallas kernels  183 us (92%)
  local copies, waits for them, and re-layouts  10.8 us (5%)
  other arithmetic  5.2 us (3%)
    pallas_call x1, Pallas kernels, layer_call(): pl.pallas_call(functools.partial(layer_kernel, shards, groups), out_shape...  183 us

profile of v1, /device:TPU:0, one launch (start us, length us, event | category | flops | bytes accessed | tf_op | source)
XLA Modules:
  0.0 198.7 jit_solution(13840370484212325361)
XLA Ops:
  0.0 0.8 subtract_subtract_fusion
  0.8 0.8 dynamic_slice.6
  1.5 0.7 add.79
  2.2 0.9 select_reduce_fusion
  3.1 0.7 sub.29.label_row_ref
  3.8 0.1 lt.44
  3.9 0.1 lt.47
  4.0 0.1 add.72
  4.1 0.7 reduce
  4.8 0.1 reshape_squeeze.3
  4.9 0.1 add.73
  5.0 0.1 add.74
  5.1 0.1 lt.48
  5.1 0.1 lt.49
  5.2 0.6 reshape.52.target_ref
  5.8 0.6 broadcast_in_dim.40.b_attention_ref
  6.5 0.9 sub.30.label_col_ref
  7.3 1.5 copy.24.keep_ref
  8.9 1.1 slice_bitcast_fusion
  9.9 1.9 concatenate.3.attention_shard_ref
  11.8 2.1 %pad_maximum_fusion.mlp_shard_ref = bf16[2,160,1280]{2,1,0:T(8,128)(2,1)} fusion(bf16[1,160,1280]{2,1,0:T(8,128)(2,1)} %bitcast.26, bf16[1,160,1280]{2,1,0:T(8,128)(2,1)} %param.26), kind=kLoop, calls=%fused_computation | loop fusion | flops 409600 | bytes 1638400 | tf_op jit(solution)/shard_map/stack | solution.py:1400
  13.9 182.7 %layer.1 = bf16[2,160,1280]{2,1,0:T(8,128)(2,1)} custom-call(bf16[8,256,1280]{2,1,0:T(8,128)(2,1)} %patches_ref.1, bf16[256,1280]{1,0:T(8,128)(2,1)} %position_ref.1, s32[8,64,1]{2,1,0:T(8,128)} %copy.24.keep_ref, s32[2,1,1024]{2,1,0:T(1,128)} %reshape.52.target_ref, s32[2,160,1]{2,1,0:T(8,128)} %sub.30.label_col_ref, s32[2,1,160]{2,1,0:T(1,128)} %sub.29.label_row_ref, ...), custom_call_target="tpu_custom_call" | custom-call | flops 99999997952 | tf_op jit(solution)/shard_map/layer/pallas_call | solution.py:1300
  196.6 2.1 %copy.27 = bf16[320,1280]{1,0:T(8,128)(2,1)} copy(bf16[320,1280]{1,0:T(8,128)(2,1)} %bitcast.25) | data formatting | bytes 1638400
  (8 shorter events, 0.0 us)

commit v2 on v1

--- a/solution.py
+++ b/solution.py
@@ -611,16 +611,17 @@
     patches_ref,
     position_ref,
     keep_ref,
-    target_ref,
-    label_col_ref,
-    label_row_ref,
+    counts_ref,
+    offsets_ref,
     gain_ref,
     shift_ref,
-    attention_shard_ref,
-    b_attention_ref,
+    w_qkv_ref,
+    b_qkv_ref,
+    w_o_ref,
     b_o_ref,
-    mlp_shard_ref,
+    w_up_ref,
     b_up_ref,
+    w_down_ref,
     b_down_ref,
     out_ref,
     patch_buf,
@@ -631,6 +632,9 @@
     w_attention,
     b_attention,
     w_mlp,
+    label_col,
+    label_row,
+    target,
     normed_ref,
     projected_ref,
     attended_ref,
@@ -648,14 +652,12 @@
     slot_recv,
     bias_send,
     bias_recv,
-    att_up,
-    att_down,
+    att_line,
     att_plane,
     att_twin,
     att_recv,
     att_twin_recv,
-    mlp_up,
-    mlp_down,
+    mlp_line,
     mlp_twin,
     mlp_recv,
     mlp_twin_recv,
@@ -677,7 +679,7 @@
     keep_most = keep_ref.shape[1]
     feature = depth // groups
     pieces, piece_rows = blocks.shape[1:3]
-    shard_rows = attention_shard_ref.shape[0]
+    shard_rows = w_up_ref.shape[0]
     half_images = images // 2
     last = planes - 1
 
@@ -695,8 +697,9 @@
         return (dp, flip(mp, k, groups))
 
     twin = (dp + 1 - 2 * core, mp)
-    above = (lax.rem(dp + 2, shards), mp)
-    below = (lax.rem(dp + shards - 2, shards), mp)
+
+    def along(distance):
+        return (lax.rem(dp + 2 * distance + shards, shards), mp)
 
     for i in range(images):
         pltpu.make_async_copy(patches_ref.at[i], patch_buf.at[i], patch_sem.at[i]).start()
@@ -714,31 +717,27 @@
         pl.semaphore_signal(barrier, inc=1, device_id=peer(k), device_id_type=MESH)
     pl.semaphore_signal(barrier, inc=1, device_id=twin, device_id_type=MESH)
 
-    @pl.when(z < last)
-    def _():
-        pl.semaphore_signal(barrier, inc=1, device_id=above, device_id_type=MESH)
-
-    @pl.when(z > 0)
-    def _():
-        pl.semaphore_signal(barrier, inc=1, device_id=below, device_id_type=MESH)
+    for distance in (-2, -1, 1, 2):
+
+        @pl.when(jnp.logical_and(z + distance >= 0, z + distance <= last))
+        def _():
+            pl.semaphore_signal(barrier, inc=1, device_id=along(distance), device_id_type=MESH)
 
     own_rows = pl.ds(pl.multiple_of(dp * shard_rows, 16), shard_rows)
-    own_att = pltpu.make_async_copy(
-        attention_shard_ref, w_attention.at[mp, own_rows, :], local_sem.at[0]
-    )
-    own_mlp = pltpu.make_async_copy(mlp_shard_ref, w_mlp.at[:, own_rows, :], local_sem.at[1])
-    own_bias = pltpu.make_async_copy(b_attention_ref, b_attention.at[mp], local_sem.at[2])
-    own_att.start()
-    own_mlp.start()
-    own_bias.start()
+    own_up = pltpu.make_async_copy(w_up_ref, w_mlp.at[0, own_rows, :], local_sem.at[0])
+    own_up.start()
+    for t in range(3):
+        at = slice(t * feature, (t + 1) * feature)
+        b_attention[mp, :, at] = jnp.broadcast_to(b_qkv_ref[t : t + 1, :], (8, feature))
+        w_attention[mp, own_rows, at] = w_qkv_ref[t]
+    w_attention[mp, own_rows, 3 * feature :] = jnp.transpose(w_o_ref[...])
     is_home = home == mp
     away = jnp.where(is_home, 0, 1)
     between = jnp.where(jnp.logical_and(z > 0, z < last), 1, 0)
-    pl.semaphore_wait(barrier, shards + groups + away + between)
-
-    own_att.wait()
-    own_mlp.wait()
-    own_bias.wait()
+    pl.semaphore_wait(barrier, shards + groups + 1 + away + between)
+
+    own_up.wait()
+    edge_plane = jnp.logical_or(z == 0, z == last)
 
     def rows_of(plane):
         return pl.ds(pl.multiple_of((2 * plane + core) * shard_rows, 16), shard_rows)
@@ -758,19 +757,45 @@
     def arrival(p):
         return by_pair(z, [row[p] for row in ARRIVALS])
 
+    def to_line(index, at, out_sems, in_sem, act):
+        for way, distance in enumerate((1, -1, 2, -2)):
+
+            @pl.when(jnp.logical_and(z + distance >= 0, z + distance <= last))
+            def _():
+                copy = remote(at, at, out_sems.at[4 * index + way], in_sem, along(distance))
+                if act:
+                    copy.start()
+                else:
+                    copy.wait_send()
+
+    def to_end(index, at, out_sems, in_sem, act):
+        for way, at_plane, distance in ((1, 1, -1), (0, last - 1, 1)):
+
+            @pl.when(z == at_plane)
+            def _():
+                copy = remote(at, at, out_sems.at[4 * index + way], in_sem, along(distance))
+                if act:
+                    copy.start()
+                else:
+                    copy.wait_send()
+
+    def att_own(act):
+        at = w_attention.at[mp, rows_of(z), :]
+        to_line(0, at, att_line, att_recv.at[mp * planes + z], act)
+
+    def att_end(act):
+        plane = arrival(last)
+        at = w_attention.at[mp, rows_of(plane), :]
+        to_end(1, at, att_line, att_recv.at[mp * planes + plane], act)
+
     def att_held(p):
         plane = arrival(p)
         if p > 0:
-            att_copy(mp, plane, att_up.at[plane], twin).wait_recv()
-
-        @pl.when(jnp.logical_and(plane <= z, z < last))
-        def _():
-            att_copy(mp, plane, att_up.at[plane], above).start()
-
-        @pl.when(jnp.logical_and(plane >= z, z > 0))
-        def _():
-            att_copy(mp, plane, att_down.at[plane], below).start()
-
+            att_copy(mp, plane, att_twin.at[0], twin).wait_recv()
+        else:
+            att_own(True)
+        if p == last:
+            att_end(True)
         att_to_twin(mp, plane).start()
 
     def att_spread(p):
@@ -782,7 +807,7 @@
         plane = arrival(p)
         for k in (1, 2):
             group = flip(mp, k, groups)
-            att_copy(group, plane, att_up.at[plane], twin).wait_recv()
+            att_copy(group, plane, att_twin.at[0], twin).wait_recv()
             if p % 2 == k - 1:
                 att_over(3 - k, group, plane, 1).start()
             att_to_twin(group, plane).start()
@@ -790,7 +815,7 @@
     def att_far(p):
         plane = arrival(p)
         group = flip(mp, 3, groups)
-        att_copy(group, plane, att_up.at[plane], twin).wait_recv()
+        att_copy(group, plane, att_twin.at[0], twin).wait_recv()
         att_to_twin(group, plane).start()
 
     def mlp_copy(j, plane, out_sem, device):
@@ -802,20 +827,23 @@
         index = j * planes + plane
         return remote(at, at, mlp_twin.at[index], mlp_twin_recv.at[index], twin)
 
+    def mlp_own(j, act):
+        at = w_mlp.at[j, rows_of(z), :]
+        to_line(2 * j, at, mlp_line, mlp_recv.at[j * planes + z], act)
+
+    def mlp_end(j, act):
+        plane = arrival(last)
+        at = w_mlp.at[j, rows_of(plane), :]
+        to_end(2 * j + 1, at, mlp_line, mlp_recv.at[j * planes + plane], act)
+
     def mlp_held(j, p):
         plane = arrival(p)
-        index = j * planes + plane
         if p > 0:
-            mlp_copy(j, plane, mlp_up.at[index], twin).wait_recv()
-
-        @pl.when(jnp.logical_and(plane <= z, z < last))
-        def _():
-            mlp_copy(j, plane, mlp_up.at[index], above).start()
-
-        @pl.when(jnp.logical_and(plane >= z, z > 0))
-        def _():
-            mlp_copy(j, plane, mlp_down.at[index], below).start()
-
+            mlp_copy(j, plane, mlp_twin.at[0], twin).wait_recv()
+        else:
+            mlp_own(j, True)
+        if p == last:
+            mlp_end(j, True)
         mlp_to_twin(j, plane).start()
 
     def bias_copy(k):
@@ -845,14 +873,15 @@
             token_recv.at[mp * half_images + i],
         )
 
-    patch_ids = lax.broadcasted_iota(jnp.int32, (keep_most, patch_count), 1)
+    patch_ids = lax.broadcasted_iota(jnp.int32, (patch_count, keep_most), 0)
 
     def pick(i):
         pltpu.make_async_copy(patches_ref.at[i], patch_buf.at[i], patch_sem.at[i]).wait()
-        chosen = (keep_ref[i] == patch_ids).astype(bf16)
-        return jnp.dot(chosen, patch_buf[i], preferred_element_type=f32) + jnp.dot(
-            chosen, position_ref[...], preferred_element_type=f32
-        )
+        chosen = (keep_ref[pl.ds(i, 1), :] == patch_ids).astype(bf16)
+        dims = (((0,), (0,)), ((), ()))
+        return lax.dot_general(
+            chosen, patch_buf[i], dims, preferred_element_type=f32
+        ) + lax.dot_general(chosen, position_ref[...], dims, preferred_element_type=f32)
 
     def some_tokens(i, carry):
         rows = pl.ds(pl.multiple_of(i * keep_most, keep_most), keep_most)
@@ -874,6 +903,52 @@
 
     lax.fori_loop(0, half_images, some_tokens, 0)
     att_spread(0)
+
+    slot_rows = 2 * slot_out.shape[1]
+    half_rows = slot_out.shape[1]
+    images_here = images * groups
+    token_count = groups * half_images * keep_most
+    lane = lax.broadcasted_iota(jnp.int32, (1, token_count), 1)
+    lane_image = lane // keep_most
+    lane_step = lane % keep_most
+    pack_rows = shards * slot_rows
+    for half in range(2):
+
+        def aim(q, row, half=half):
+            image = dp * images_here + (q // half_images) * images + half * half_images
+            image = image + q % half_images
+            offset = offsets_ref[image]
+            live = jnp.logical_and(lane_image == q, lane_step < counts_ref[image])
+            return jnp.where(live, offset + lane_step, row)
+
+        row = lax.fori_loop(
+            0, groups * half_images, aim, jnp.full((1, token_count), -1, jnp.int32)
+        )
+        target[half] = row
+
+    for j in range(per):
+        first = dp * pack_rows + (mp * per + j) * slot_rows
+        row_at = first + lax.broadcasted_iota(jnp.int32, (1, slot_rows), 1)
+        col_at = first + lax.broadcasted_iota(jnp.int32, (slot_rows, 128), 0)
+
+        def tell(q, found, j=j, row_at=row_at, col_at=col_at):
+            in_row, in_col = found
+            image = (mp * per + j) * images_here + q
+            low = offsets_ref[image]
+            high = low + counts_ref[image]
+            in_row = jnp.where(jnp.logical_and(row_at >= low, row_at < high), image, in_row)
+            in_col = jnp.where(jnp.logical_and(col_at >= low, col_at < high), image, in_col)
+            return in_row, in_col
+
+        none = (
+            jnp.full((1, slot_rows), -1, jnp.int32),
+            jnp.full((slot_rows, 128), -1, jnp.int32),
+        )
+        in_row, in_col = lax.fori_loop(0, images_here, tell, none)
+        label_row[j] = in_row
+        label_col[j] = in_col
+
+    w_mlp[1, own_rows, :] = jnp.transpose(w_down_ref[...])
     att_held(1)
     att_spread(1)
 
@@ -910,17 +985,16 @@
         slot = lax.rem(dp, per) * groups + mp
         return pltpu.make_async_copy(slot_out.at[dp], slot_in.at[slot], slot_recv.at[slot])
 
-    slot_rows = 2 * slot_out.shape[1]
-    half_rows = slot_out.shape[1]
-    token_count = groups * half_images * keep_most
     edge = feature // 128 * 128
     width = feature - edge + feature
 
     def place(i, carry):
-        first = 2 * i * slot_rows
-        rows = first + lax.broadcasted_iota(jnp.int32, (2 * slot_rows, token_count), 0)
-        left = (rows == target_ref[0]).astype(bf16)
-        right = (rows == target_ref[1]).astype(bf16)
+        row = lax.broadcasted_iota(jnp.int32, (2 * slot_rows, token_count), 0)
+        below = row < slot_rows
+        first = 2 * i * pack_rows + dp * slot_rows
+        rows = row + jnp.where(below, first, first + pack_rows - slot_rows)
+        left = (rows == target[0]).astype(bf16)
+        right = (rows == target[1]).astype(bf16)
         tokens = token_in[...].reshape(token_count, 2 * feature)
         whole = (
             jnp.dot(left, tokens[:, :width], preferred_element_type=f32)[:, :feature]
@@ -947,10 +1021,21 @@
     lax.fori_loop(0, shards // 2, place, 0)
     att_held(2)
     att_spread(2)
+
+    @pl.when(jnp.logical_not(edge_plane))
+    def _():
+        att_held(3)
+        att_spread(3)
+
+    mlp_held(0, 0)
     att_near(0)
-    att_held(3)
-    att_spread(3)
-    mlp_held(0, 0)
+
+    @pl.when(edge_plane)
+    def _():
+        att_held(3)
+        att_spread(3)
+
+    att_near(1)
 
     for j in range(per):
         for g in range(groups):
@@ -982,11 +1067,11 @@
         def put(low):
             whole = jnp.concatenate(
                 [
-                    slot_in[j * groups + g, rows, :].astype(f32)[:, low : low + feature]
+                    slot_in[j * groups + g, rows, :][:, low : low + feature]
                     for g in range(groups)
                 ],
                 axis=-1,
-            )
+            ).astype(f32)
             to = pl.ds(pl.multiple_of(i * rows_tile, rows_tile), rows_tile)
             residual_ref[to, :] = whole + b_o_ref[...]
             normed_ref[to, :] = norm_rows(whole, gain_ref[0:1], shift_ref[0:1])
@@ -1002,7 +1087,7 @@
         return carry
 
     lax.fori_loop(0, 2 * per * steps, assemble, 0)
-    mlp_held(0, 1)
+    att_near(2)
 
     heads = feature // HEAD
     scale = 1.0 / math.sqrt(HEAD)
@@ -1017,23 +1102,22 @@
 
         @pl.when(step == 1)
         def _():
+            mlp_held(0, 1)
+            att_near(3)
+            mlp_held(1, 0)
             mlp_held(0, 2)
-            for p in range(1, planes):
-                att_near(p)
-            mlp_held(0, 3)
-            mlp_held(1, 0)
             att_far(0)
             att_far(1)
 
-        @pl.when(step == 2)
-        def _():
-            mlp_held(1, 1)
+        @pl.when(jnp.logical_and(step == 2, jnp.logical_not(edge_plane)))
+        def _():
+            mlp_held(0, 3)
 
         @pl.when(step == 3)
         def _():
             att_far(2)
             att_far(3)
-            mlp_held(1, 2)
+            mlp_held(1, 1)
 
         @pl.when(step > 0)
         def _():
@@ -1061,7 +1145,7 @@
             key = projected_ref[rows, low_key : 2 * feature].astype(f32)[:, feature - low_key :]
             key = key.astype(bf16)
             value = projected_ref[rows, 2 * feature : used]
-            matches = label_col_ref[j] == label_row_ref[j]
+            matches = label_col[j][:, 0:1] == label_row[j]
             spans = [(t, min(t + 128, feature)) for t in range(0, feature, 128)]
             totals = [jnp.zeros((slot_rows, high - low), f32) for low, high in spans]
             for h in range(heads):
@@ -1122,103 +1206,130 @@
 
         lax.fori_loop(0, piece_rows // norm_tile, norm_some, 0)
 
+    def slot_of(k, h):
+        return k if h == 0 or k in (0, 3) else 3 - k
+
     def out_copy(k, h):
-        at = k * pieces + h
-        return remote(blocks.at[0, h], blocks.at[k, h], send_a.at[at], recv_a.at[at], peer(k))
+        q = slot_of(k, h)
+        at = q * pieces + h
+        return remote(blocks.at[0, h], blocks.at[q, h], send_a.at[at], recv_a.at[at], peer(k))
 
     def back_copy(k, h):
-        at = k * pieces + h
-        return remote(parts.at[k, h], backs.at[k, h], send_b.at[at], recv_b.at[at], peer(k))
+        q = slot_of(k, h)
+        at = q * pieces + h
+        return remote(parts.at[q, h], backs.at[q, h], send_b.at[at], recv_b.at[at], peer(k))
 
     def forward(h):
-        held, k = (1, 2) if h == 0 else (2, 1)
         at = 3 * pieces + h
-        return remote(blocks.at[held, h], blocks.at[3, h], send_a.at[at], recv_a.at[at], peer(k))
+        return remote(blocks.at[1, h], blocks.at[3, h], send_a.at[at], recv_a.at[at], peer(2 - h))
 
     def across(h):
         at = 3 * pieces + h
         return remote(parts.at[3, h], relay.at[h], send_b.at[at], recv_b.at[at], peer(1 + h))
 
-    for k, h in ((1, 0), (2, 1), (1, 1), (2, 0)):
+    first_pair = ((1, 0), (2, 1))
+    second_pair = ((1, 1), (2, 0))
+    for k, h in first_pair + second_pair:
         out_copy(k, h).start()
-    mlp_held(1, 3)
-    for j in range(2):
+
+    @pl.when(edge_plane)
+    def _():
+        mlp_held(0, 3)
+
+    def mlp_here(j):
         for plane in range(planes):
             at = w_mlp.at[0, pl.ds(0, shard_rows), :]
             remote(
                 at, at, mlp_twin.at[0], mlp_twin_recv.at[j * planes + plane], twin
             ).wait_recv()
 
+    mlp_here(0)
+    pair_rows = pieces * piece_rows
+
     def mlp_step(i, carry):
-        late = (i + 2) // 8
-        middle = ((i + 2) // 4) % 2
-        k = middle * (1 + i % 2) + 3 * late
-        h = (i // 4 + i % 2) % 2
+        q = lax.rem(i + 1, 4)
+
+        @pl.when(i == 0)
+        def _():
+            mlp_held(1, 2)
+
+            @pl.when(jnp.logical_not(edge_plane))
+            def _():
+                mlp_held(1, 3)
+
+            for k, h in first_pair:
+                out_copy(k, h).wait_recv()
+            forward(0).start()
+            forward(1).start()
+
+        @pl.when(i == 1)
+        def _():
+            for k, h in second_pair:
+                out_copy(k, h).wait_recv()
 
         @pl.when(i == 2)
         def _():
-            out_copy(1, 0).wait_recv()
-            forward(0).start()
-            out_copy(2, 1).wait_recv()
-            forward(1).start()
-
-        @pl.when(i >= 4)
-        def _():
-            out_copy(k, h).wait_recv()
+            for h in range(2):
+                forward(h).wait_recv()
 
         def up(t, carry):
             at = pl.ds(pl.multiple_of(t * column, column), column)
-            y = jnp.dot(blocks[k, h], w_mlp[0, :, at], preferred_element_type=f32) + b_up_ref[:, at]
+            x = blocks[q].reshape(pair_rows, depth)
+            y = jnp.dot(x, w_mlp[0, :, at], preferred_element_type=f32) + b_up_ref[:, at]
             y = 0.5 * y * (1.0 + lax.erf(y * math.sqrt(0.5)))
             hidden_ref[:, at] = y.astype(bf16)
             return carry
 
         lax.fori_loop(0, hidden_ref.shape[1] // column, up, 0)
 
+        @pl.when(i == 0)
+        def _():
+            @pl.when(edge_plane)
+            def _():
+                mlp_held(1, 3)
+
+            mlp_here(1)
+
         def down(t, carry):
             at = pl.ds(pl.multiple_of(t * column, column), column)
-            parts[k, h, :, at] = lax.dot_general(
+            y = lax.dot_general(
                 hidden_ref[...],
                 w_mlp[1, at, :],
                 (((1,), (1,)), ((), ())),
                 preferred_element_type=f32,
             ).astype(bf16)
+            for h in range(pieces):
+                parts[q, h, :, at] = y[h * piece_rows : (h + 1) * piece_rows]
             return carry
 
         lax.fori_loop(0, depth // column, down, 0)
 
+        @pl.when(i == 0)
+        def _():
+            for k, h in first_pair:
+                back_copy(k, h).start()
+
         @pl.when(i == 2)
         def _():
-            back_copy(1, 0).start()
-
-        @pl.when(i == 3)
-        def _():
-            back_copy(2, 1).start()
-
-        @pl.when(i == 6)
-        def _():
-            across(1).start()
-
-        @pl.when(i == 7)
-        def _():
-            across(0).start()
+            for h in range(2):
+                across(h).start()
 
         return carry
 
-    lax.fori_loop(0, 8, mlp_step, 0)
-    for h, k in ((1, 1), (0, 2)):
+    lax.fori_loop(0, 4, mlp_step, 0)
+    for k, h in second_pair:
         across(h).wait_recv()
 
-        def add(i, carry, h=h, k=k):
+        def add(i, carry, h=h):
             rows = pl.ds(pl.multiple_of(i * norm_tile, norm_tile), norm_tile)
-            parts[k, h, rows, :] = (
-                parts[k, h, rows, :].astype(f32) + relay[h, rows, :].astype(f32)
+            parts[2, h, rows, :] = (
+                parts[2, h, rows, :].astype(f32) + relay[h, rows, :].astype(f32)
             ).astype(bf16)
             return carry
 
         lax.fori_loop(0, piece_rows // norm_tile, add, 0)
         back_copy(k, h).start()
-    for k, h in ((1, 0), (2, 1), (1, 1), (2, 0)):
+    for k, h in first_pair + second_pair:
         back_copy(k, h).wait_recv()
     for h in range(pieces):
 
@@ -1226,10 +1337,10 @@
             rows = pl.ds(pl.multiple_of(i * norm_tile, norm_tile), norm_tile)
             at = pl.ds(pl.multiple_of(h * piece_rows + i * norm_tile, norm_tile), norm_tile)
             total = residual_ref[at, :] + b_down_ref[...] + parts[0, h, rows, :].astype(f32)
-            for k in (1, 2):
-                total = total + backs[k, h, rows, :].astype(f32)
-            live = label_col_ref[h, rows, :] >= 0
-            out_ref[h, rows, :] = jnp.where(live, total, 0.0).astype(bf16)
+            for q in (1, 2):
+                total = total + backs[q, h, rows, :].astype(f32)
+            live = label_col[h, rows, :][:, 0:1] >= 0
+            out_ref[at, :] = jnp.where(live, total, 0.0).astype(bf16)
             return carry
 
         lax.fori_loop(0, piece_rows // norm_tile, finish, 0)
@@ -1257,21 +1368,13 @@
         return carry
 
     lax.fori_loop(0, shards, slot_sent, 0)
+    att_own(False)
+    att_end(False)
+    for j in range(2):
+        mlp_own(j, False)
+        mlp_end(j, False)
     for p in range(planes):
         plane = arrival(p)
-
-        @pl.when(jnp.logical_and(plane <= z, z < last))
-        def _():
-            att_copy(mp, plane, att_up.at[plane], above).wait_send()
-            for j in range(2):
-                mlp_copy(j, plane, mlp_up.at[j * planes + plane], above).wait_send()
-
-        @pl.when(jnp.logical_and(plane >= z, z > 0))
-        def _():
-            att_copy(mp, plane, att_down.at[plane], below).wait_send()
-            for j in range(2):
-                mlp_copy(j, plane, mlp_down.at[j * planes + plane], below).wait_send()
-
         for g in range(groups):
             att_to_twin(g, plane).wait_send()
         for j in range(2):
@@ -1280,76 +1383,6 @@
             att_over(k, mp, plane, 0).wait_send()
         k = 1 + p % 2
         att_over(3 - k, flip(mp, k, groups), plane, 1).wait_send()
-
-
-def layer_call(shards, groups, args, slot_rows):
-    patches, keep, attention_shard, mlp_shard = args[0], args[2], args[8], args[11]
-    images, _, depth = patches.shape
-    keep_most = keep.shape[1]
-    feature = depth // groups
-    per = shards // groups
-    rows = per * slot_rows
-    planes = shards // 2
-    half_images = images // 2
-    vmem = pl.BlockSpec(memory_space=pltpu.VMEM)
-    bf16 = jnp.bfloat16
-    hidden = mlp_shard.shape[2]
-    dma = pltpu.SemaphoreType.DMA
-    buffer = pltpu.VMEM((groups, per, slot_rows, depth), bf16)
-    used = 3 * feature
-    return pl.pallas_call(
-        functools.partial(layer_kernel, shards, groups),
-        out_shape=jax.ShapeDtypeStruct((per, slot_rows, depth), bf16),
-        in_specs=[pl.BlockSpec(memory_space=pl.ANY)] + [vmem] * (len(args) - 1),
-        out_specs=vmem,
-        scratch_shapes=[
-            pltpu.VMEM(patches.shape, bf16),
-            pltpu.VMEM((groups, half_images * keep_most, 2 * feature), bf16),
-            pltpu.VMEM((groups, half_images * keep_most, 2 * feature), bf16),
-            pltpu.VMEM((shards, slot_rows // 2, 2 * feature), bf16),
-            pltpu.VMEM((shards, slot_rows // 2, 2 * feature), bf16),
-            pltpu.VMEM((groups, shards * attention_shard.shape[0], attention_shard.shape[1]), bf16),
-            pltpu.VMEM((groups,) + args[9].shape, jnp.float32),
-            pltpu.VMEM((2, shards * mlp_shard.shape[1], hidden), bf16),
-            pltpu.VMEM((rows, depth), bf16),
-            pltpu.VMEM((rows, args[9].shape[1]), bf16),
-            pltpu.VMEM((rows, attention_shard.shape[1] - used // 128 * 128), bf16),
-            pltpu.VMEM((rows, depth), jnp.float32),
-            buffer,
-            buffer,
-            buffer,
-            pltpu.VMEM((per, slot_rows, depth), bf16),
-            pltpu.VMEM((slot_rows, hidden), bf16),
-            dma((images,)),
-            dma((3,)),
-            dma((groups * half_images,)),
-            dma((groups * half_images,)),
-            dma((shards,)),
-            dma((shards,)),
-            dma((groups,)),
-            dma((groups,)),
-            dma((planes,)),
-            dma((planes,)),
-            dma((6 * planes,)),
-            dma((groups * planes,)),
-            dma((groups * planes,)),
-            dma((groups * planes,)),
-            dma((2 * planes,)),
-            dma((2 * planes,)),
-            dma((2 * planes,)),
-            dma((2 * planes,)),
-            dma((2 * planes,)),
-            dma((groups * per,)),
-            dma((groups * per,)),
-            dma((groups * per,)),
-            dma((groups * per,)),
-        ],
-        compiler_params=pltpu.CompilerParams(
-            collective_id=3, has_side_effects=True, vmem_limit_bytes=60 * 1024 * 1024
-        ),
-        cost_estimate=pl.CostEstimate(flops=100_000_000_000, bytes_accessed=0, transcendentals=0),
-        name="layer",
-    )(*args)
 
 
 def one_kernel(
@@ -1369,59 +1402,96 @@
     w_down,
     b_down,
 ):
-    local_images, _, depth = patches.shape
+    images, _, depth = patches.shape
     keep_most = keep.shape[1]
     shards = lax.axis_size("dp")
     groups = lax.axis_size("mp")
-    images_here = local_images * groups
-    slot_rows = slot_size(images_here, shards, keep_most)
-    pack_rows = slot_rows * shards
+    slot_rows = slot_size(images * groups, shards, keep_most)
     per = shards // groups
-    dp = lax.axis_index("dp")
-    mp = lax.axis_index("mp")
     feature = depth // groups
-
-    own_counts = lax.dynamic_slice_in_dim(counts, dp * images_here, images_here)
-    own_offsets = lax.dynamic_slice_in_dim(offsets, dp * images_here, images_here)
-    shard = own_offsets // pack_rows
-    base = shard * slot_rows + own_offsets - shard * pack_rows - dp * slot_rows
-    step = jnp.arange(keep_most, dtype=jnp.int32)
-    target = jnp.where(step[None, :] < own_counts[:, None], base[:, None] + step[None, :], -1)
-    target = target.reshape(groups, 2, -1).transpose(1, 0, 2).reshape(2, 1, -1)
-
-    first = dp * pack_rows + mp * per * slot_rows
-    rows = first + jnp.arange(per * slot_rows, dtype=jnp.int32)
-    inside = (rows[:, None] >= offsets[None, :]) & (rows[:, None] < (offsets + counts)[None, :])
-    image_ids = jnp.arange(counts.shape[0], dtype=jnp.int32)
-    labels = jnp.max(jnp.where(inside, image_ids[None, :] + 1, 0), axis=1) - 1
-    labels = labels.reshape(per, slot_rows)
-
-    attention_shard = jnp.concatenate([w_qkv[0, 0], w_qkv[0, 1], w_qkv[0, 2], w_o[0].T], axis=1)
-    mlp_shard = jnp.stack([w_up[0], w_down[0].T])
-    bias = b_qkv[0].reshape(1, -1)
-    pad = (3 * feature + 255) // 256 * 256 - 3 * feature
-    bias = jnp.broadcast_to(jnp.pad(bias, ((0, 0), (0, pad))), (8, 3 * feature + pad))
-    return layer_call(
-        shards,
-        groups,
-        (
-            patches,
-            position,
-            keep[:, :, None],
-            target,
-            labels[:, :, None],
-            labels[:, None, :],
-            ln_gain[0],
-            ln_bias[0],
-            attention_shard,
-            bias,
-            b_o,
-            mlp_shard,
-            b_up,
-            b_down,
+    planes = shards // 2
+    rows = per * slot_rows
+    used = 3 * feature
+    padded = (used + 255) // 256 * 256
+    hidden = w_up.shape[2]
+    shard_width = used + w_o.shape[1]
+    some = (images // 2) * keep_most
+    bf16 = jnp.bfloat16
+    i32 = jnp.int32
+    vmem = pl.BlockSpec(memory_space=pltpu.VMEM)
+    smem = pl.BlockSpec(memory_space=pltpu.SMEM)
+    dma = pltpu.SemaphoreType.DMA
+    buffer = pltpu.VMEM((groups, per, slot_rows, depth), bf16)
+    return pl.pallas_call(
+        functools.partial(layer_kernel, shards, groups),
+        out_shape=jax.ShapeDtypeStruct((rows, depth), bf16),
+        in_specs=[pl.BlockSpec(memory_space=pl.ANY), vmem, vmem, smem, smem] + [vmem] * 10,
+        out_specs=vmem,
+        scratch_shapes=[
+            pltpu.VMEM(patches.shape, bf16),
+            pltpu.VMEM((groups, some, 2 * feature), bf16),
+            pltpu.VMEM((groups, some, 2 * feature), bf16),
+            pltpu.VMEM((shards, slot_rows // 2, 2 * feature), bf16),
+            pltpu.VMEM((shards, slot_rows // 2, 2 * feature), bf16),
+            pltpu.VMEM((groups, depth, shard_width), bf16),
+            pltpu.VMEM((groups, 8, padded), jnp.float32),
+            pltpu.VMEM((2, depth, hidden), bf16),
+            pltpu.VMEM((per, slot_rows, 128), i32),
+            pltpu.VMEM((per, 1, slot_rows), i32),
+            pltpu.VMEM((2, 1, groups * some), i32),
+            pltpu.VMEM((rows, depth), bf16),
+            pltpu.VMEM((rows, padded), bf16),
+            pltpu.VMEM((rows, shard_width - used // 128 * 128), bf16),
+            pltpu.VMEM((rows, depth), jnp.float32),
+            buffer,
+            buffer,
+            buffer,
+            pltpu.VMEM((per, slot_rows, depth), bf16),
+            pltpu.VMEM((rows, hidden), bf16),
+            dma((images,)),
+            dma((1,)),
+            dma((groups * images // 2,)),
+            dma((groups * images // 2,)),
+            dma((shards,)),
+            dma((shards,)),
+            dma((groups,)),
+            dma((groups,)),
+            dma((8,)),
+            dma((6 * planes,)),
+            dma((groups * planes,)),
+            dma((groups * planes,)),
+            dma((groups * planes,)),
+            dma((16,)),
+            dma((2 * planes,)),
+            dma((2 * planes,)),
+            dma((2 * planes,)),
+            dma((groups * per,)),
+            dma((groups * per,)),
+            dma((groups * per,)),
+            dma((groups * per,)),
+        ],
+        compiler_params=pltpu.CompilerParams(
+            collective_id=3, has_side_effects=True, vmem_limit_bytes=60 * 1024 * 1024
         ),
-        slot_rows,
-    ).reshape(per * slot_rows, depth)
+        cost_estimate=pl.CostEstimate(flops=100_000_000_000, bytes_accessed=0, transcendentals=0),
+        name="layer",
+    )(
+        patches,
+        position,
+        keep,
+        counts,
+        offsets,
+        ln_gain[0],
+        ln_bias[0],
+        w_qkv[0],
+        b_qkv[0],
+        w_o[0],
+        b_o,
+        w_up[0],
+        b_up,
+        w_down[0],
+        b_down,
+    )
 
 
 def solution(mesh):

time: 199 us -> 170 us (0.85)
  Pallas kernels: 183 us -> 163 us
  other arithmetic: 5.2 us -> 0 us
  local copies, waits for them, and re-layouts: 10.8 us -> 7.13 us
    pallas_call x1, Pallas kernels: 183 us -> 163 us  [one_kernel(): pl.pallas_call(functools.partial(layer_kernel, shards, groups), out_shape...]
    unnamed x1 -> x4, local copies, waits for them, and re-layouts: 2.09 us -> 7.13 us
    broadcast_in_dim x2 -> x0, local copies, waits for them, and re-layouts: 2.16 us -> none  [the longest x1 1.55 us: one_kernel(): keep[:, :, None]]
    another operation x1 -> x0, other arithmetic: 2.09 us -> none  [one_kernel(): mlp_shard = jnp.stack([w_up[0], w_down[0].T])]
where the time goes in v2:
time: 170 us
  Pallas kernels  163 us (96%)
  local copies, waits for them, and re-layouts  7.13 us (4%)
    pallas_call x1, Pallas kernels, one_kernel(): pl.pallas_call(functools.partial(layer_kernel, shards, groups), out_shape...  163 us
    unnamed x4, local copies, waits for them, and re-layouts  7.13 us

profile of v2, /device:TPU:0, one launch (start us, length us, event | category | flops | bytes accessed | tf_op | source)
XLA Modules:
  0.0 169.7 jit_solution(5820895617363889291)
XLA Ops:
  0.0 1.3 copy.20
  1.3 1.7 copy.16
  3.0 2.1 %copy.17 = bf16[1,1280,160]{2,1,0:T(8,128)(2,1)} copy(bf16[1,1280,160]{1,2,0:T(8,128)(2,1)} %param.28) | data formatting | bytes 819200 | tf_op args[13]
  5.0 162.6 %layer.1 = bf16[320,1280]{1,0:T(8,128)(2,1)} custom-call(bf16[8,256,1280]{2,1,0:T(8,128)(2,1)} %patches_ref.1, bf16[256,1280]{1,0:T(8,128)(2,1)} %position_ref.1, s32[8,64]{1,0:T(8,128)} %keep_ref.1, s32[256]{0:T(256)} %counts_ref.1, s32[256]{0:T(256)} %offsets_ref.1, f32[2,1280]{1,0:T(2,128)} %bitcast.14, f32[2,1280]{1,0:T(2,128)} %bitcast.15, ...), custom_call_target="tpu_custom_call" | custom-call | flops 99999997952 | tf_op jit(solution)/shard_map/layer/pallas_call | solution.py:1425
  167.6 2.1 %copy.22 = bf16[320,1280]{1,0:T(8,128)(2,1)} copy(bf16[320,1280]{1,0:T(8,128)(2,1)} %layer.1) | data formatting | bytes 1638400
